TPU v7x, 32 devices: a 4x4x1 block of a 4x4x8 slice. The times are simulated.
32 devices in a mesh: data: 1 (over z), pp: 4 (over y), ep: 8 (over x, core).
Axes of the slice: x: 4, y: 4, z: 1, core: 2. Of those that a mesh axis runs over, the one named last changes fastest.
The devices are a block of a 4x4x8 slice.
Arguments:
- expert_out: bfloat16 [4, 1, 64, 320, 2048], P(('data', 'pp'), None, 'ep')
- expert_id: int32 [4, 1, 2048, 8], P(('data', 'pp'), None, 'ep')
- slot_id: int32 [4, 1, 2048, 8], P(('data', 'pp'), None, 'ep')
- gate: float32 [4, 1, 2048, 8], P(('data', 'pp'), None, 'ep')
- resid: bfloat16 [4, 1, 2048, 2048], P(('data', 'pp'), None, 'ep')
- owner: int32 [4, 64], P(('data', 'pp'))
- norm_w: float32 [4, 2048], P('pp')
- w_q: bfloat16 [4, 2048, 2048], P('pp')
- w_k: bfloat16 [4, 2048, 2048], P('pp')
- w_v: bfloat16 [4, 2048, 2048], P('pp')
- w_o: bfloat16 [4, 2048, 2048], P('pp')
Outputs:
- output: bfloat16 [4, 1, 2048, 2048], P(('data', 'pp'), None, 'ep')
All inputs are finite; a program needn't handle non-finite values.
Results may differ from a plain program's by a relative error of at most 0.0140715.
Values are sent between devices in bfloat16 or wider.
A program may use at most 768 MiB of HBM per device.

v0:
```python
import jax
import jax.numpy as jnp
from jax import lax
from jax.sharding import PartitionSpec as P

HEAD_DIM = 128
NORM_EPS = 1e-6


def attend_local(y_owned, norm_scale, w_q, w_k, w_v, w_o):
    n_micro, n_seqs, seq_len, model_dim = y_owned.shape
    n_heads = w_q.shape[1] // HEAD_DIM
    y_f32 = y_owned.astype(jnp.float32)
    inv_rms = lax.rsqrt(jnp.mean(y_f32 * y_f32, axis=-1, keepdims=True) + NORM_EPS)
    normed = (y_f32 * inv_rms * norm_scale).astype(jnp.bfloat16)

    def project(weight):
        proj_out = jnp.einsum('msld,de->msle', normed, weight, preferred_element_type=jnp.float32)
        return proj_out.astype(jnp.bfloat16).reshape(n_micro, n_seqs, seq_len, n_heads, HEAD_DIM)

    queries = project(w_q)
    key_vecs = project(w_k)
    values = project(w_v)
    scores = jnp.einsum('msqhe,mskhe->mshqk', queries, key_vecs, preferred_element_type=jnp.float32) * (HEAD_DIM ** -0.5)
    causal = jnp.arange(seq_len)[:, None] >= jnp.arange(seq_len)[None, :]
    attn_probs = jax.nn.softmax(jnp.where(causal, scores, -1e30), axis=-1).astype(jnp.bfloat16)
    head_mix = jnp.einsum('mshqk,mskhe->msqhe', attn_probs, values, preferred_element_type=jnp.float32).astype(jnp.bfloat16)
    out_proj = jnp.einsum('msqhe,hed->msqd', head_mix, w_o.reshape(n_heads, HEAD_DIM, model_dim), preferred_element_type=jnp.float32)
    return (y_f32 + out_proj.astype(jnp.bfloat16).astype(jnp.float32)).astype(jnp.bfloat16)


def combine_home(recv_out, expert_id, slot_id, gate, resid, dev_index, cap_dev):
    n_micro = recv_out.shape[0]
    model_dim = recv_out.shape[3]
    kept_mask = slot_id >= 0
    local_slot = jnp.where(kept_mask, slot_id - dev_index * cap_dev, 0)
    row_index = expert_id * cap_dev + local_slot
    flat_out = recv_out.reshape(n_micro, -1, model_dim)
    picked = jax.vmap(lambda out_table, row_ids: out_table[row_ids])(flat_out, row_index)
    weights = jnp.where(kept_mask, gate, 0.0)
    combined = jnp.sum(picked.astype(jnp.float32) * weights[..., None], axis=2)
    return (resid.astype(jnp.float32) + combined).astype(jnp.bfloat16)


def solution(mesh):
    n_stages = mesh.shape['pp']
    n_ep = mesh.shape['ep']
    next_rank = [(src_rank, (src_rank + 1) % n_stages) for src_rank in range(n_stages)]
    group_axes = ('data', 'pp')

    def device_step(expert_out, expert_id, slot_id, gate, resid, owner, norm_w, w_q, w_k, w_v, w_o):
        dev_index = lax.axis_index('ep')
        out_local = expert_out[0]
        cap_dev = out_local.shape[2] // n_ep
        recv_out = lax.all_to_all(out_local, 'ep', 2, 1, tiled=True)
        y_home = combine_home(recv_out, expert_id[0], slot_id[0], gate[0], resid[0], dev_index, cap_dev)
        y_next = lax.ppermute(y_home, 'pp', next_rank)
        n_micro, tok_dev, model_dim = y_next.shape
        seq_dev = owner.shape[1] // n_ep
        per_pair = seq_dev // n_ep
        owner_grid = owner[0].reshape(n_ep, seq_dev)
        src_dev = owner_grid // seq_dev
        positions = jnp.arange(seq_dev)
        send_rank = jnp.argsort(jnp.where(src_dev == dev_index, 0, seq_dev) + positions, axis=1)[:, :per_pair]
        send_seq = jnp.take_along_axis(owner_grid, send_rank, axis=1).reshape(seq_dev) - dev_index * seq_dev
        y_seqs = y_next.reshape(n_micro, seq_dev, tok_dev // seq_dev, model_dim)
        outgoing = jnp.take(y_seqs, send_seq, axis=1)
        incoming = lax.all_to_all(outgoing, 'ep', 1, 1, tiled=True)
        my_src = lax.dynamic_index_in_dim(src_dev, dev_index, 0, keepdims=False)
        arrival = jnp.argsort(my_src * seq_dev + positions)
        y_owned = jnp.take(incoming, jnp.argsort(arrival), axis=1)
        z_owned = attend_local(y_owned, norm_w[0], w_q[0], w_k[0], w_v[0], w_o[0])
        return z_owned.reshape(n_micro, tok_dev, model_dim)[None]

    tok_spec = P(group_axes, None, 'ep', None)
    weight_spec = P('pp', None, None)
    in_specs = (P(group_axes, None, 'ep', None, None), tok_spec, tok_spec, tok_spec, tok_spec, P(group_axes, None), P('pp', None), weight_spec, weight_spec, weight_spec, weight_spec)
    return jax.shard_map(device_step, mesh=mesh, in_specs=in_specs, out_specs=tok_spec, check_vma=False)
```

profile of v0, /device:TPU:97, one launch (start us, length us, event | category | flops | bytes accessed | tf_op | source)
XLA Modules:
  0.0 287.8 jit_solution(4934154247950900284)
XLA Ops:
  0.0 13.6 %copy.87 = bf16[1,1,8,320,2048]{4,2,3,1,0:T(8,128)(2,1)} copy(bf16[1,1,8,320,2048]{4,3,2,1,0:T(8,128)(2,1)} %param.13) | data formatting | bytes 20971520 | tf_op args[0]
  13.6 7.2 %all-to-all-start = ((bf16[1,8,320,2048]{3,1,0,2:T(8,128)(2,1)}), bf16[1,8,320,2048]{3,1,0,2:T(8,128)(2,1)}, u32[]{:S(2)}, u32[]{:S(2)}) async-start(bf16[1,8,320,2048]{3,1,0,2:T(8,128)(2,1)} %bitcast.156), calls=%async_computation | async-start | bytes 20971520 | tf_op jit(solution)/shard_map/all_to_all | solution.py:55
  20.9 0.1 copy.46
  21.0 0.1 reshape.272
  21.2 0.1 copy.47
  21.3 0.5 broadcast.254
  21.8 0.7 reduce.11
  22.5 0.1 reshape_squeeze.6
  22.5 0.1 copy.40
  22.6 114.3 %all-to-all-done = bf16[1,8,320,2048]{3,1,0,2:T(8,128)(2,1)} async-done(((bf16[1,8,320,2048]{3,1,0,2:T(8,128)(2,1)}), bf16[1,8,320,2048]{3,1,0,2:T(8,128)(2,1)}, u32[]{:S(2)}, u32[]{:S(2)}) %all-to-all-start) | async-done | bytes 10485792 | tf_op jit(solution)/shard_map/all_to_all | solution.py:55
  136.9 14.7 %copy.45 = bf16[1,8,8,40,2048]{4,3,1,2,0:T(8,128)(2,1)} copy(bf16[1,8,8,40,2048]{4,1,3,2,0:T(8,128)(2,1)} %bitcast.7) | data formatting | bytes 20971520 | tf_op jit(solution)/shard_map/all_to_all | solution.py:55
  151.7 48.9 %gather_fusion = bf16[2048,2048]{1,0:T(8,128)(2,1)} fusion(bf16[1,2560,2048]{2,1,0:T(8,128)(2,1)} %bitcast.155, s32[2048]{0:T(1024)S(1)} %reshape.272), kind=kCustom, calls=%fused_computation.2 | custom fusion | bytes 16793600 | tf_op jit(solution)/shard_map/vmap()/gather | solution.py:39
  200.5 11.4 %fusion.1 = f32[256,2048]{1,0:T(8,128)S(1)} fusion(bf16[2048,2048]{1,0:T(8,128)(2,1)} %gather_fusion, f32[256,8]{1,0:T(8,128)S(1)} %copy.47), kind=kLoop, calls=%fused_computation.6 | loop fusion | flops 12058624 | bytes 10493952 | tf_op jit(solution)/shard_map/reduce_sum | solution.py:41
  212.0 1.3 fusion.24
  213.2 1.0 collective-permute-start
  214.3 0.7 sort.48
  215.0 0.6 gather_fusion.1
  215.6 23.9 %collective-permute-done = bf16[1,256,2048]{2,1,0:T(8,128)(2,1)S(1)} collective-permute-done((bf16[1,256,2048]{2,1,0:T(8,128)(2,1)}, bf16[1,256,2048]{2,1,0:T(8,128)(2,1)S(1)}, u32[]{:S(2)}, u32[]{:S(2)}) %collective-permute-start) | collective-permute-done | bytes 1048608 | tf_op jit(solution)/shard_map/ppermute | solution.py:57
  239.5 0.6 gather_fusion.2
  240.1 1.1 bitcast_select_fusion.1
  241.3 4.9 %all-to-all-start.1 = ((bf16[1,8,32,2048]{3,2,0,1:T(8,128)(2,1)}), bf16[1,8,32,2048]{3,2,0,1:T(8,128)(2,1)S(1)}, u32[]{:S(2)}, u32[]{:S(2)}) async-start(bf16[1,8,32,2048]{3,2,0,1:T(8,128)(2,1)} %bitcast_select_fusion.1), calls=%async_computation.1 | async-start | bytes 2097152 | tf_op jit(solution)/shard_map/all_to_all | solution.py:68
  246.2 0.2 multiply_reduce_fusion
  246.4 1.0 sort.49
  247.5 1.0 sort.50
  248.5 12.5 %all-to-all-done.1 = bf16[1,8,32,2048]{3,2,0,1:T(8,128)(2,1)S(1)} async-done(((bf16[1,8,32,2048]{3,2,0,1:T(8,128)(2,1)}), bf16[1,8,32,2048]{3,2,0,1:T(8,128)(2,1)S(1)}, u32[]{:S(2)}, u32[]{:S(2)}) %all-to-all-start.1) | async-done | bytes 1048608 | tf_op jit(solution)/shard_map/all_to_all | solution.py:68
  261.1 0.6 gather_fusion.3
  261.7 0.4 fusion.21
  262.1 5.9 %fusion.27 = bf16[8,4,16,8,128]{4,3,2,1,0:T(8,128)(2,1)S(1)} fusion(bf16[1,2048,2048]{2,1,0:T(8,128)(2,1)} %param.21, f32[2048]{0:T(1024)S(1)} %bitcast.162, f32[8,32]{1,0:T(8,128)S(1)} %add_rsqrt_fusion, bf16[8,32,2048]{2,1,0:T(8,128)(2,1)S(1)} %gather_fusion.3, pred[8]{0:T(512)(128)(4,1)S(1)} %compare_and_fusion), kind=kOutput, calls=%fused_computation.36 | convolution fusion | flops 2150629376 | bytes 10494984 | tf_op jit(solution)/shard_map/msld,de->msle/dot_general | solution.py:18
  268.1 5.9 %fusion.30 = bf16[8,4,16,8,128]{4,3,2,1,0:T(8,128)(2,1)S(1)} fusion(bf16[1,2048,2048]{2,1,0:T(8,128)(2,1)} %param.20, f32[2048]{0:T(1024)S(1)} %bitcast.163, f32[8,32]{1,0:T(8,128)S(1)} %add_rsqrt_fusion, bf16[8,32,2048]{2,1,0:T(8,128)(2,1)S(1)} %gather_fusion.3, pred[8]{0:T(512)(128)(4,1)S(1)} %compare_and_fusion), kind=kOutput, calls=%fused_computation.37 | convolution fusion | flops 2150629376 | bytes 10494984 | tf_op jit(solution)/shard_map/msld,de->msle/dot_general | solution.py:18
  274.0 3.4 %fusion.33 = bf16[8,4,16,8,128]{4,3,2,1,0:T(8,128)(2,1)} fusion(bf16[1,2048,2048]{2,1,0:T(8,128)(2,1)S(1)} %bitcast.160, f32[2048]{0:T(1024)S(1)} %bitcast.164, f32[8,32]{1,0:T(8,128)S(1)} %add_rsqrt_fusion, bf16[8,32,2048]{2,1,0:T(8,128)(2,1)S(1)} %gather_fusion.3, pred[8]{0:T(512)(128)(4,1)S(1)} %compare_and_fusion), kind=kOutput, calls=%fused_computation.38 | convolution fusion | flops 2150629376 | bytes 10494984 | tf_op jit(solution)/shard_map/msld,de->msle/dot_general | solution.py:18
  277.4 2.3 fusion.74
  279.7 8.1 %fusion.20 = bf16[1,8,32,2048]{3,2,1,0:T(8,128)(2,1)} fusion(bf16[16,128,2048,1]{2,1,0,3:T(8,128)(2,1)} %bitcast.161, f32[8,16,32,32]{2,3,1,0:T(8,128)} %get-tuple-element.17, bf16[8,4,16,8,128]{4,3,2,1,0:T(8,128)(2,1)} %fusion.33, f32[8,16,32]{2,1,0:T(8,128)S(1)} %get-tuple-element.16, bf16[8,32,2048]{2,1,0:T(8,128)(2,1)S(1)} %gather_fusion.3, ...), kind=kOutput, calls=%fused_computation.24 | convolution fusion | flops 2184970240 | bytes 12075016 | tf_op jit(solution)/shard_map/msqhe,hed->msqd/dot_general | solution.py:28
  (37 shorter events, 0.2 us)
Async XLA Ops:
  13.6 7.2 %copy-start.1 = (s32[1,1,256,8]{2,3,1,0:T(8,128)S(1)}, s32[1,1,256,8]{2,3,1,0:T(8,128)}, u32[]{:S(2)}) copy-start(s32[1,1,256,8]{2,3,1,0:T(8,128)} %param.15) | copy-start | bytes 24580
  13.6 7.2 %copy-start.2 = (s32[1,1,256,8]{2,3,1,0:T(8,128)S(1)}, s32[1,1,256,8]{2,3,1,0:T(8,128)}, u32[]{:S(2)}) copy-start(s32[1,1,256,8]{2,3,1,0:T(8,128)} %param.14) | copy-start | bytes 24580
  13.6 7.5 %copy-start.3 = (f32[1,1,256,8]{2,3,1,0:T(8,128)S(1)}, f32[1,1,256,8]{2,3,1,0:T(8,128)}, u32[]{:S(2)}) copy-start(f32[1,1,256,8]{2,3,1,0:T(8,128)} %param.16) | copy-start | bytes 24580
  13.6 8.2 %copy-start.5 = (s32[1,64]{1,0:T(1,128)S(1)}, s32[1,64]{1,0:T(1,128)}, u32[]{:S(2)}) copy-start(s32[1,64]{1,0:T(1,128)} %param.18) | copy-start | bytes 772
  13.6 123.3 %all-to-all-start = ((bf16[1,8,320,2048]{3,1,0,2:T(8,128)(2,1)}), bf16[1,8,320,2048]{3,1,0,2:T(8,128)(2,1)}, u32[]{:S(2)}, u32[]{:S(2)}) async-start(bf16[1,8,320,2048]{3,1,0,2:T(8,128)(2,1)} %bitcast.156), calls=%async_computation | async-start | bytes 20971520 | tf_op jit(solution)/shard_map/all_to_all | solution.py:55
  200.5 11.4 %copy-start = (bf16[1,1,256,2048]{3,2,1,0:T(8,128)(2,1)S(1)}, bf16[1,1,256,2048]{3,2,1,0:T(8,128)(2,1)}, u32[]{:S(2)}) copy-start(bf16[1,1,256,2048]{3,2,1,0:T(8,128)(2,1)} %param.17) | copy-start | bytes 3145732
  213.2 26.3 %collective-permute-start = (bf16[1,256,2048]{2,1,0:T(8,128)(2,1)}, bf16[1,256,2048]{2,1,0:T(8,128)(2,1)S(1)}, u32[]{:S(2)}, u32[]{:S(2)}) collective-permute-start(bf16[1,256,2048]{2,1,0:T(8,128)(2,1)} %fusion.24), channel_id=1, source_target_pairs={{0,8},{8,16},{16,24},{24,0},{1,9},{9,17},{17,25},{25,1},{2,10},{10... | collective-permute-start | bytes 3145736 | tf_op jit(solution)/shard_map/ppermute | solution.py:57
  241.3 19.8 %all-to-all-start.1 = ((bf16[1,8,32,2048]{3,2,0,1:T(8,128)(2,1)}), bf16[1,8,32,2048]{3,2,0,1:T(8,128)(2,1)S(1)}, u32[]{:S(2)}, u32[]{:S(2)}) async-start(bf16[1,8,32,2048]{3,2,0,1:T(8,128)(2,1)} %bitcast_select_fusion.1), calls=%async_computation.1 | async-start | bytes 2097152 | tf_op jit(solution)/shard_map/all_to_all | solution.py:68
  246.2 15.9 %copy-start.4 = (f32[1,2048]{1,0:T(1,128)S(1)}, f32[1,2048]{1,0:T(1,128)}, u32[]{:S(2)}) copy-start(f32[1,2048]{1,0:T(1,128)} %param.19) | copy-start | bytes 24580
  262.1 11.9 %slice-start = ((s8[8388608]{0:T(1024)(128)(4,1)}), s8[4194304]{0:T(1024)(128)(4,1)S(1)}, s32[]{:S(2)}) async-start(s8[8388608]{0:T(1024)(128)(4,1)} %bitcast.159), calls=%async_computation.2 | async-start | bytes 8388608
  268.1 6.0 %slice-start.1 = ((s8[8388608]{0:T(1024)(128)(4,1)}), s8[4194304]{0:T(1024)(128)(4,1)S(1)}, s32[]{:S(2)}) async-start(s8[8388608]{0:T(1024)(128)(4,1)} %bitcast.159), calls=%async_computation.3 | async-start | bytes 8388608
where the time goes:
time: 289 us; the launch traced here: 288 us
  waiting for transfers between devices  151 us (52%)
  local copies, waits for them, and re-layouts  80.2 us (28%)
  matrix products  25.6 us (9%)
  other arithmetic  17.9 us (6%)
  starting transfers between devices  13.2 us (5%)
    all_to_all x1, waiting for transfers between devices, device_step(): recv_out = lax.all_to_all(out_local, 'ep', 2, 1, tiled=True)  114 us
    gather x4, local copies, waits for them, and re-layouts, combine_home(): out_table[row_ids]  49.1 us
    ppermute x1, waiting for transfers between devices, device_step(): y_next = lax.ppermute(y_home, 'pp', next_rank)  23.9 us
    dot_general x3, matrix products, project(): jnp.einsum('msld,de->msle', normed, weight, preferred_element_type=jnp.fl...  15.2 us
    all_to_all x1, local copies, waits for them, and re-layouts, device_step(): recv_out = lax.all_to_all(out_local, 'ep', 2, 1, tiled=True)  14.7 us
    unnamed x19, local copies, waits for them, and re-layouts  14.2 us
    all_to_all x1, waiting for transfers between devices, device_step(): incoming = lax.all_to_all(outgoing, 'ep', 1, 1, tiled=True)  12.5 us
    reduce_sum x1, other arithmetic, combine_home(): combined = jnp.sum(picked.astype(jnp.float32) * weights[..., None], axis=2)  11.4 us
  transfers between devices with their start and end apart: 3, of which 3 were waited for; matrix products, arithmetic and copies ran while one was open for 2% of the time, Pallas kernels for 0%

commit v1 on v0

v1 whole, which is shorter than its diff:
```python
import functools

import jax
import jax.numpy as jnp
from jax import lax
from jax.experimental import pallas as pl
from jax.experimental.pallas import tpu as pltpu
from jax.sharding import PartitionSpec as P

HEAD_DIM = 128
NORM_EPS = 1e-6
MESH = pl.DeviceIdType.MESH
CORES = 2


def attend_local(y_owned, norm_scale, w_q, w_k, w_v, w_o):
    n_micro, n_seqs, seq_len, model_dim = y_owned.shape
    n_heads = w_q.shape[1] // HEAD_DIM
    y_f32 = y_owned.astype(jnp.float32)
    inv_rms = lax.rsqrt(jnp.mean(y_f32 * y_f32, axis=-1, keepdims=True) + NORM_EPS)
    normed = (y_f32 * inv_rms * norm_scale).astype(jnp.bfloat16)

    def project(weight):
        proj_out = jnp.einsum('msld,de->msle', normed, weight, preferred_element_type=jnp.float32)
        return proj_out.astype(jnp.bfloat16).reshape(n_micro, n_seqs, seq_len, n_heads, HEAD_DIM)

    queries = project(w_q)
    key_vecs = project(w_k)
    values = project(w_v)
    scores = jnp.einsum('msqhe,mskhe->mshqk', queries, key_vecs, preferred_element_type=jnp.float32) * (HEAD_DIM ** -0.5)
    causal = jnp.arange(seq_len)[:, None] >= jnp.arange(seq_len)[None, :]
    attn_probs = jax.nn.softmax(jnp.where(causal, scores, -1e30), axis=-1).astype(jnp.bfloat16)
    head_mix = jnp.einsum('mshqk,mskhe->msqhe', attn_probs, values, preferred_element_type=jnp.float32).astype(jnp.bfloat16)
    out_proj = jnp.einsum('msqhe,hed->msqd', head_mix, w_o.reshape(n_heads, HEAD_DIM, model_dim), preferred_element_type=jnp.float32)
    return (y_f32 + out_proj.astype(jnp.bfloat16).astype(jnp.float32)).astype(jnp.bfloat16)


def combine_kernel(dims, route_ref, out_ref, resid_ref, y_ref,
                   obuf, hbuf, routes, table, wterm, p1, p2, p3, r1, r2, r3, own, ysend, yland,
                   o_loc, o_snd, o_rcv, h_loc, h_snd, h_rcv, t_loc, t_snd, t_rcv,
                   s1, s2, s3, q1, q2, q3, ys, yr):
    n_ep, n_st, n_loc, cap, slot_pad, seq_len, top_k, half = dims
    n_chip = n_ep // CORES
    n_half = n_ep // 2
    tok_dev = n_ep * seq_len
    me = lax.axis_index('ep')
    rank = lax.axis_index('pp')
    core = lax.rem(me, CORES)
    chip = me // CORES
    sib = me + 1 - 2 * core
    nxt = lax.rem(rank + 1, n_st)
    prv = lax.rem(rank + n_st - 1, n_st)
    side = [lax.rem(me + n_ep - CORES, n_ep), lax.rem(me + CORES, n_ep)]
    my_cols = pl.ds(pl.multiple_of(core * half, 128), half)
    sib_cols = pl.ds(pl.multiple_of((1 - core) * half, 128), half)

    loc = []
    for h in range(n_ep):
        loc.append(pltpu.make_async_copy(out_ref.at[:, pl.ds(h * cap, cap), my_cols],
                                         obuf.at[h, pl.ds(core * n_loc, n_loc), pl.ds(0, cap)], o_loc.at[h]))
        loc[-1].start()
    h_copy = pltpu.make_async_copy(resid_ref.at[:, my_cols], hbuf.at[core], h_loc)
    h_copy.start()
    t_copy = pltpu.make_async_copy(route_ref, routes.at[me], t_loc)
    t_copy.start()

    barrier = pltpu.get_barrier_semaphore()
    for k in range(1, n_ep):
        pl.semaphore_signal(barrier, inc=1, device_id={'ep': lax.rem(me + k, n_ep)}, device_id_type=MESH)
    for other in (nxt, prv):
        for jc in range(CORES):
            pl.semaphore_signal(barrier, inc=1, device_id={'pp': other, 'ep': chip * CORES + jc}, device_id_type=MESH)
    if slot_pad > cap:
        for h in range(n_ep):
            obuf[h, :, cap:, :] = jnp.zeros((CORES * n_loc, slot_pad - cap, half), jnp.bfloat16)
    pl.semaphore_wait(barrier, n_ep - 1 + 2 * CORES)

    t_out = []
    for k in range(1, n_ep):
        peer = lax.rem(me + k, n_ep)
        t_out.append(pltpu.make_async_remote_copy(route_ref, routes.at[me], t_snd.at[k - 1], t_rcv.at[me],
                                                  device_id={'ep': peer}, device_id_type=MESH))
        t_out[-1].start()
    o_out = []
    for h in range(n_ep):
        o_out.append(pltpu.make_async_remote_copy(out_ref.at[:, pl.ds(h * cap, cap), sib_cols],
                                                  obuf.at[h, pl.ds(core * n_loc, n_loc), pl.ds(0, cap)],
                                                  o_snd.at[h], o_rcv.at[h],
                                                  device_id={'ep': sib}, device_id_type=MESH))
        o_out[-1].start()
    h_out = pltpu.make_async_remote_copy(resid_ref.at[:, sib_cols], hbuf.at[core], h_snd, h_rcv,
                                         device_id={'ep': sib}, device_id_type=MESH)
    h_out.start()

    t_copy.wait()
    for k in range(1, n_ep):
        src = lax.rem(me + k, n_ep)
        pltpu.make_async_remote_copy(route_ref, routes.at[src], t_snd.at[k - 1], t_rcv.at[src],
                                     device_id={'ep': src}, device_id_type=MESH).wait_recv()
    h_copy.wait()
    h_out.wait_recv()

    def o_wait(h):
        pltpu.make_async_copy(out_ref.at[:, pl.ds(0, cap), my_cols],
                              obuf.at[h, pl.ds(core * n_loc, n_loc), pl.ds(0, cap)], o_loc.at[h]).wait()
        pltpu.make_async_remote_copy(out_ref.at[:, pl.ds(0, cap), sib_cols],
                                     obuf.at[h, pl.ds((1 - core) * n_loc, n_loc), pl.ds(0, cap)],
                                     o_snd.at[h], o_rcv.at[h],
                                     device_id={'ep': sib}, device_id_type=MESH).wait_recv()

    depth = CORES * n_loc * slot_pad
    width = min(256, half)
    lane = lax.broadcasted_iota(jnp.int32, (seq_len, depth), 1).astype(jnp.float32)
    block = CORES * seq_len

    def partial(q, ab):
        h = q + n_half * ab
        o_wait(h)
        rows = routes[h]
        rows = jnp.concatenate([rows, jnp.zeros((128 - rows.shape[0], tok_dev), jnp.float32)], axis=0)
        table[...] = rows.T
        step = 1 - 2 * ab
        dest = [chip + 2, chip + n_chip + step, chip + n_chip - step, chip]
        picks = []
        for r in range(n_chip):
            for jc in range(CORES):
                j = lax.rem(dest[r], n_chip) * CORES + jc
                picks.append(pl.multiple_of(j * seq_len, seq_len))
        base = (chip * depth).astype(jnp.float32)
        for b, start in enumerate(picks):
            rt = table[pl.ds(start, seq_len), :]
            w = jnp.zeros((seq_len, depth), jnp.float32)
            for j in range(top_k):
                key = rt[:, j:j + 1] - base
                w = jnp.where(lane == key, rt[:, top_k + j:top_k + j + 1], w)
            hi = w.astype(jnp.bfloat16)
            rest = w - hi.astype(jnp.float32)
            mid = rest.astype(jnp.bfloat16)
            low = (rest - mid.astype(jnp.float32)).astype(jnp.bfloat16)
            for t, term in enumerate((hi, mid, low)):
                wterm[pl.ds(t * tok_dev + b * seq_len, seq_len), :] = term

        dsts = [p1.at[ab, q], p2.at[1 - ab, q], p3.at[ab, q], own.at[ab, q]]

        @pl.loop(0, half // width)
        def _(n):
            cols = pl.ds(pl.multiple_of(n * width, width), width)
            slots = obuf[h, :, :, cols].reshape(depth, width)
            res = jnp.dot(wterm[...], slots, preferred_element_type=jnp.float32)
            res = res[:tok_dev] + (res[tok_dev:2 * tok_dev] + res[2 * tok_dev:])
            for r in range(n_chip):
                dsts[r][:, cols] = res[r * block:(r + 1) * block]

        @pl.when(h // CORES == chip)
        def _():
            hc = lax.rem(h, CORES)
            for b, start in enumerate(picks):
                dst = dsts[b // CORES]
                rs = slice((b % CORES) * seq_len, (b % CORES + 1) * seq_len)
                dst[rs, :] = dst[rs, :] + hbuf[hc, pl.ds(start, seq_len), :].astype(jnp.float32)

    def ring(src, dst, snd, rcv, d, q):
        return pltpu.make_async_remote_copy(src.at[d, q], dst.at[d, q], snd.at[d, q], rcv.at[d, q],
                                            device_id={'ep': side[d]}, device_id_type=MESH)

    def hop(q, jc):
        return pltpu.make_async_remote_copy(ysend.at[q, jc], yland.at[pl.ds(2 * q, 2), :, my_cols],
                                            ys.at[q, jc], yr.at[core, q],
                                            device_id={'pp': nxt, 'ep': chip * CORES + jc}, device_id_type=MESH)

    @pl.loop(0, n_half + 2)
    def _(it):
        @pl.when(it < n_half)
        def _():
            @pl.loop(0, 2)
            def _(ab):
                partial(it, ab)
            for d in range(2):
                ring(p1, r1, s1, q1, d, it).start()

        @pl.when(jnp.logical_and(it >= 1, it <= n_half))
        def _():
            q = it - 1
            for d in range(2):
                ring(p2, r2, s2, q2, d, q).start()
            for d in range(2):
                ring(p1, r1, s1, q1, d, q).wait_recv()
                p3[d, q] = p3[d, q] + r1[d, q]
                ring(p3, r3, s3, q3, d, q).start()

        @pl.when(it >= 2)
        def _():
            q = it - 2
            for d in range(2):
                ring(p2, r2, s2, q2, d, q).wait_recv()
                ring(p3, r3, s3, q3, d, q).wait_recv()
            for ab in range(2):
                total = own[ab, q] + (r3[ab, q] + r2[1 - ab, q])
                rounded = total.astype(jnp.bfloat16)
                for jc in range(CORES):
                    ysend[q, jc, ab] = rounded[jc * seq_len:(jc + 1) * seq_len]
            for jc in range(CORES):
                hop(q, jc).start()

    @pl.loop(0, n_half)
    def _(q):
        for c in range(CORES):
            cols = pl.ds(c * half, half)
            pltpu.make_async_remote_copy(ysend.at[q, 0], yland.at[pl.ds(2 * q, 2), :, cols],
                                         ys.at[q, 0], yr.at[c, q],
                                         device_id={'pp': nxt, 'ep': me}, device_id_type=MESH).wait_recv()
    y_ref[...] = yland[...]

    for k in range(1, n_ep):
        t_out[k - 1].wait_send()
    for h in range(n_ep):
        o_out[h].wait_send()
    h_out.wait_send()

    @pl.loop(0, n_half)
    def _(q):
        for d in range(2):
            ring(p1, r1, s1, q1, d, q).wait_send()
            ring(p2, r2, s2, q2, d, q).wait_send()
            ring(p3, r3, s3, q3, d, q).wait_send()
        for jc in range(CORES):
            hop(q, jc).wait_send()


def solution(mesh):
    n_stages = mesh.shape['pp']
    n_ep = mesh.shape['ep']
    prev_rank = [((src_rank + 1) % n_stages, src_rank) for src_rank in range(n_stages)]
    group_axes = ('data', 'pp')

    def device_step(expert_out, expert_id, slot_id, gate, resid, owner, norm_w, w_q, w_k, w_v, w_o):
        dev_index = lax.axis_index('ep')
        n_loc, capacity, model_dim = expert_out.shape[2:]
        cap = capacity // n_ep
        tok_dev, top_k = expert_id.shape[2:]
        seq_dev = owner.shape[1] // n_ep
        seq_len = tok_dev // seq_dev
        assert expert_out.shape[1] == 1 and seq_dev == n_ep
        half = model_dim // CORES
        slot_pad = -(-cap // 16) * 16
        n_half = n_ep // 2
        block = CORES * seq_len

        grid = owner[0].reshape(n_ep, seq_dev)
        homes = jnp.arange(n_ep)[:, None, None]
        pick = jnp.sum(jnp.where(grid[None] // seq_dev == homes, grid[None] - homes * seq_dev, 0), axis=2)
        pick = lax.ppermute(pick.reshape(-1).astype(jnp.int32), 'pp', prev_rank)
        my_src = lax.dynamic_index_in_dim(grid // seq_dev, dev_index, 0, keepdims=False)
        pos = (my_src % n_half * 2 + my_src // n_half).astype(jnp.int32)

        key = jnp.where(slot_id[0, 0] >= 0, expert_id[0, 0] * slot_pad + slot_id[0, 0] - dev_index * cap, -1)
        leaving = lax.dynamic_index_in_dim(pick.reshape(n_ep, n_ep), dev_index, 0, keepdims=False)
        route = jnp.concatenate([key.astype(jnp.float32), gate[0, 0]], axis=1)
        route = jnp.take(route.reshape(seq_dev, seq_len, 2 * top_k), leaving, axis=0).reshape(tok_dev, 2 * top_k).T
        held = jnp.take(resid[0, 0].reshape(seq_dev, seq_len, model_dim), leaving, axis=0).reshape(tok_dev, model_dim)

        dims = (n_ep, n_stages, n_loc, cap, slot_pad, seq_len, top_k, half)
        f32, bf16 = jnp.float32, jnp.bfloat16
        ringbuf = pltpu.VMEM((2, n_half, block, half), f32)
        dma = pltpu.SemaphoreType.DMA
        y_owned = pl.pallas_call(
            functools.partial(combine_kernel, dims),
            out_shape=jax.ShapeDtypeStruct((n_ep, seq_len, model_dim), bf16),
            in_specs=[pl.BlockSpec(memory_space=pltpu.VMEM)] + [pl.BlockSpec(memory_space=pl.ANY)] * 2,
            out_specs=pl.BlockSpec(memory_space=pltpu.VMEM),
            scratch_shapes=[
                pltpu.VMEM((n_ep, CORES * n_loc, slot_pad, half), bf16),
                pltpu.VMEM((CORES, tok_dev, half), bf16),
                pltpu.VMEM((n_ep, 2 * top_k, tok_dev), f32),
                pltpu.VMEM((tok_dev, 128), f32),
                pltpu.VMEM((3 * tok_dev, CORES * n_loc * slot_pad), bf16),
                ringbuf, ringbuf, ringbuf, ringbuf, ringbuf, ringbuf, ringbuf,
                pltpu.VMEM((n_half, CORES, 2, seq_len, half), bf16),
                pltpu.VMEM((n_ep, seq_len, model_dim), bf16),
                dma((n_ep,)), dma((n_ep,)), dma((n_ep,)),
                dma, dma, dma,
                dma, dma((n_ep - 1,)), dma((n_ep,)),
                dma((2, n_half)), dma((2, n_half)), dma((2, n_half)),
                dma((2, n_half)), dma((2, n_half)), dma((2, n_half)),
                dma((n_half, CORES)), dma((CORES, n_half)),
            ],
            compiler_params=pltpu.CompilerParams(collective_id=0, has_side_effects=True, vmem_limit_bytes=60 * 2 ** 20),
            name='combine',
        )(route, expert_out[0, 0], held)
        y_owned = jnp.take(y_owned, pos, axis=0)
        z_owned = attend_local(y_owned[None], norm_w[0], w_q[0], w_k[0], w_v[0], w_o[0])
        return z_owned.reshape(1, tok_dev, model_dim)[None]

    tok_spec = P(group_axes, None, 'ep', None)
    weight_spec = P('pp', None, None)
    in_specs = (P(group_axes, None, 'ep', None, None), tok_spec, tok_spec, tok_spec, tok_spec, P(group_axes, None), P('pp', None), weight_spec, weight_spec, weight_spec, weight_spec)
    return jax.shard_map(device_step, mesh=mesh, in_specs=in_specs, out_specs=tok_spec, check_vma=False)
```

time: 289 us -> 141 us (0.49)
  waiting for transfers between devices: 151 us -> 0.01 us
  Pallas kernels: 0 us -> 101 us
  local copies, waits for them, and re-layouts: 80.2 us -> 4.93 us
  other arithmetic: 17.9 us -> 4.59 us
  starting transfers between devices: 13.2 us -> 5.22 us
    all_to_all x2 -> x0, waiting for transfers between devices: 127 us -> none  [the longest x1 114 us: device_step(): recv_out = lax.all_to_all(out_local, 'ep', 2, 1, tiled=True)]
    pallas_call x0 -> x1, Pallas kernels: none -> 101 us  [device_step(): pl.pallas_call(functools.partial(combine_kernel, dims), out_shape=jax.Sha...]
    gather x7 -> x5, local copies, waits for them, and re-layouts: 51 us -> 3.12 us  [the longest x1 1.84 us: device_step(): y_owned = jnp.take(y_owned, pos, axis=0)]
    ppermute x1, waiting for transfers between devices: 23.9 us -> 0.01 us  [device_step(): pick = lax.ppermute(pick.reshape(-1).astype(jnp.int32), 'pp', prev_rank)]
    all_to_all x1 -> x0, local copies, waits for them, and re-layouts: 14.7 us -> none  [device_step(): recv_out = lax.all_to_all(out_local, 'ep', 2, 1, tiled=True)]
    unnamed x19 -> x13, local copies, waits for them, and re-layouts: 14.2 us -> 0.55 us
    all_to_all x2 -> x0, starting transfers between devices: 12.1 us -> none  [the longest x1 7.2 us: device_step(): recv_out = lax.all_to_all(out_local, 'ep', 2, 1, tiled=True)]
    reduce_sum x1, other arithmetic: 11.4 us -> 0.28 us  [device_step(): jnp.sum(jnp.where(grid[None] // seq_dev == homes, grid[None] - homes * se...]
  transfers between devices with their start and end apart: 3 -> 1, of which waited for: 3 -> 0; matrix products, arithmetic and copies ran while one was open for 2% -> 1% of each run, Pallas kernels for 0% -> 0%
where the time goes in v1:
time: 141 us; the launch traced here: 140 us
  Pallas kernels  101 us (72%)
  matrix products  24.6 us (17%)
  starting transfers between devices  5.22 us (4%)
  local copies, waits for them, and re-layouts  4.93 us (3%)
  other arithmetic  4.59 us (3%)
    pallas_call x1, Pallas kernels, device_step(): pl.pallas_call(functools.partial(combine_kernel, dims), out_shape=jax.Sha...  101 us
    dot_general x3, matrix products, project(): jnp.einsum('msld,de->msle', normed, weight, preferred_element_type=jnp.fl...  12.9 us
    dot_general x1, matrix products, attend_local(): jnp.einsum('msqhe,hed->msqd', head_mix, w_o.reshape(n_heads, HEAD_DIM, mo...  8.1 us
    ppermute x1, starting transfers between devices, device_step(): pick = lax.ppermute(pick.reshape(-1).astype(jnp.int32), 'pp', prev_rank)  5.22 us
    sub x1, matrix products, attend_local(): jax.nn.softmax(jnp.where(causal, scores, -1e+30), axis=-1)  3.56 us
  transfers between devices with their start and end apart: 1, of which 0 were waited for; matrix products, arithmetic and copies ran while one was open for 1% of the time, Pallas kernels for 0%

profile of v1, /device:TPU:97, one launch (start us, length us, event | category | flops | bytes accessed | tf_op | source)
XLA Modules:
  0.0 140.5 jit_solution(12626074388196780701)
XLA Ops:
  0.0 0.5 broadcast.186
  0.5 1.3 reduce.9
  1.8 0.1 broadcast_in_dim_reshape_squeeze.4
  1.9 0.3 select_reduce_fusion
  2.2 0.1 reshape.212
  2.3 5.2 %collective-permute-start = (s32[64]{0:T(128)S(1)}, s32[64]{0:T(128)S(1)}, u32[]{:S(2)}, u32[]{:S(2)}) collective-permute-start(s32[64]{0:T(128)S(1)} %reshape.212), channel_id=1, source_target_pairs={{8,0},{16,8},{24,16},{0,24},{9,1},{17,9},{25,17},{1,25},{10,2},{18... | collective-permute-start | bytes 776 | tf_op jit(solution)/shard_map/ppermute | solution.py:252
  7.5 0.7 select_convert_fusion
  8.3 0.1 reshape.219
  8.4 0.8 concatenate.6
  9.2 0.0 collective-permute-done
  9.2 0.1 reshape.213
  9.3 0.1 broadcast_in_dim.47
  9.4 0.1 broadcast_in_dim.48
  9.5 0.6 gather_fusion
  10.1 0.1 gather.10
  10.2 0.6 gather_fusion.1
  10.8 1.1 broadcast_select_fusion.1
  11.9 0.6 select_bitcast_fusion.route_ref
  12.5 101.0 %combine.1 = bf16[8,32,2048]{2,1,0:T(8,128)(2,1)} custom-call(f32[16,256]{1,0:T(8,128)} %select_bitcast_fusion.route_ref, bf16[8,320,2048]{2,1,0:T(8,128)(2,1)} %bitcast.120, bf16[256,2048]{1,0:T(8,128)(2,1)} %bitcast.121), custom_call_target="tpu_custom_call" | custom-call | tf_op jit(solution)/shard_map/combine/pallas_call | solution.py:266
  113.6 0.0 copy-start.1
  113.6 1.8 %gather_fusion.2 = bf16[8,32,2048]{2,1,0:T(8,128)(2,1)S(1)} fusion(bf16[8,32,2048]{2,1,0:T(8,128)(2,1)} %combine.1, s32[1024]{0:T(1024)S(1)} %pad_clamp_fusion), kind=kCustom, calls=%fused_computation.1.clone | custom fusion | bytes 2097184 | tf_op jit(solution)/shard_map/jit(_take)/gather | solution.py:290
  115.4 0.0 slice-start
  115.4 0.4 fusion.19
  115.9 0.0 copy-done.1
  115.9 0.0 slice-start.2
  115.9 6.0 %fusion.27 = bf16[8,4,16,8,128]{4,3,2,1,0:T(8,128)(2,1)S(1)} fusion(bf16[1,2048,2048]{2,1,0:T(8,128)(2,1)} %param.20, f32[2048]{0:T(1024)S(1)} %bitcast.127, f32[8,32]{1,0:T(8,128)S(1)} %add_rsqrt_fusion, bf16[8,32,2048]{2,1,0:T(8,128)(2,1)S(1)} %gather_fusion.2, pred[8]{0:T(512)(128)(4,1)S(1)} %get-tuple-element.6), kind=kOutput, calls=%fused_computation.30 | convolution fusion | flops 2150629376 | bytes 10494984 | tf_op jit(solution)/shard_map/msld,de->msle/dot_general | solution.py:24
  121.9 0.0 slice-start.3
  122.0 3.4 %fusion.24 = bf16[8,4,16,8,128]{4,3,2,1,0:T(8,128)(2,1)} fusion(bf16[1,2048,2048]{2,1,0:T(8,128)(2,1)S(1)} %bitcast.123, f32[2048]{0:T(1024)S(1)} %bitcast.128, f32[8,32]{1,0:T(8,128)S(1)} %add_rsqrt_fusion, bf16[8,32,2048]{2,1,0:T(8,128)(2,1)S(1)} %gather_fusion.2, pred[8]{0:T(512)(128)(4,1)S(1)} %get-tuple-element.6), kind=kOutput, calls=%fused_computation.29 | convolution fusion | flops 2150629376 | bytes 10494984 | tf_op jit(solution)/shard_map/msld,de->msle/dot_general | solution.py:24
  125.4 0.0 slice-done.2
  125.4 3.4 %fusion.30 = bf16[8,4,16,8,128]{4,3,2,1,0:T(8,128)(2,1)} fusion(bf16[1,2048,2048]{2,1,0:T(8,128)(2,1)S(1)} %bitcast.125, f32[2048]{0:T(1024)S(1)} %bitcast.129, f32[8,32]{1,0:T(8,128)S(1)} %add_rsqrt_fusion, bf16[8,32,2048]{2,1,0:T(8,128)(2,1)S(1)} %gather_fusion.2, pred[8]{0:T(512)(128)(4,1)S(1)} %get-tuple-element.6), kind=kOutput, calls=%fused_computation.31 | convolution fusion | flops 2150629376 | bytes 10494984 | tf_op jit(solution)/shard_map/msld,de->msle/dot_general | solution.py:24
  128.8 3.6 %fusion.69 = (f32[8,16,32]{2,1,0:T(8,128)S(1)}, f32[8,16,32,32]{2,3,1,0:T(8,128)}) fusion(pred[32,32]{0,1:T(8,128)(4,1)S(1)} %iota_compare_fusion.1, bf16[8,4,16,8,128]{4,3,2,1,0:T(8,128)(2,1)} %fusion.24, bf16[8,4,16,8,128]{4,3,2,1,0:T(8,128)(2,1)S(1)} %fusion.27), kind=kOutput, calls=%fused_computation.80 | convolution fusion | flops 34078752 | bytes 2638848 | tf_op jit(solution)/shard_map/sub | solution.py:32
  132.4 8.1 %fusion.9 = bf16[8,32,2048]{2,1,0:T(8,128)(2,1)} fusion(bf16[16,128,2048,1]{2,1,0,3:T(8,128)(2,1)} %bitcast.126, f32[8,16,32,32]{2,3,1,0:T(8,128)} %get-tuple-element.11, bf16[8,4,16,8,128]{4,3,2,1,0:T(8,128)(2,1)} %fusion.30, f32[8,16,32]{2,1,0:T(8,128)S(1)} %get-tuple-element.10, bf16[8,32,2048]{2,1,0:T(8,128)(2,1)S(1)} %gather_fusion.2, ...), kind=kOutput, calls=%fused_computation.16 | convolution fusion | flops 2184970240 | bytes 12075016 | tf_op jit(solution)/shard_map/msqhe,hed->msqd/dot_general | solution.py:34
  (22 shorter events, 0.2 us)
Async XLA Ops:
  0.0 10.2 %copy-start = (bf16[1,1,256,2048]{3,2,1,0:T(8,128)(2,1)S(1)}, bf16[1,1,256,2048]{3,2,1,0:T(8,128)(2,1)}, u32[]{:S(2)}) copy-start(bf16[1,1,256,2048]{3,2,1,0:T(8,128)(2,1)} %param.17) | copy-start | bytes 3145732
  2.3 6.9 %collective-permute-start = (s32[64]{0:T(128)S(1)}, s32[64]{0:T(128)S(1)}, u32[]{:S(2)}, u32[]{:S(2)}) collective-permute-start(s32[64]{0:T(128)S(1)} %reshape.212), channel_id=1, source_target_pairs={{8,0},{16,8},{24,16},{0,24},{9,1},{17,9},{25,17},{1,25},{10,2},{18... | collective-permute-start | bytes 776 | tf_op jit(solution)/shard_map/ppermute | solution.py:252
  113.6 2.3 %copy-start.1 = (f32[1,2048]{1,0:T(1,128)S(1)}, f32[1,2048]{1,0:T(1,128)}, u32[]{:S(2)}) copy-start(f32[1,2048]{1,0:T(1,128)} %param.19) | copy-start | bytes 24580
  115.4 6.5 %slice-start = ((s8[8388608]{0:T(1024)(128)(4,1)}), s8[4194304]{0:T(1024)(128)(4,1)S(1)}, s32[]{:S(2)}) async-start(s8[8388608]{0:T(1024)(128)(4,1)} %bitcast.122), calls=%async_computation | async-start | bytes 8388608
  115.9 6.1 %slice-start.1 = ((s8[8388608]{0:T(1024)(128)(4,1)}), s8[4194304]{0:T(1024)(128)(4,1)S(1)}, s32[]{:S(2)}) async-start(s8[8388608]{0:T(1024)(128)(4,1)} %bitcast.122), calls=%async_computation.1 | async-start | bytes 8388608
  115.9 9.5 %slice-start.2 = ((s8[8388608]{0:T(1024)(128)(4,1)}), s8[4194304]{0:T(1024)(128)(4,1)S(1)}, s32[]{:S(2)}) async-start(s8[8388608]{0:T(1024)(128)(4,1)} %bitcast.124), calls=%async_computation.2 | async-start | bytes 8388608
  121.9 3.5 %slice-start.3 = ((s8[8388608]{0:T(1024)(128)(4,1)}), s8[4194304]{0:T(1024)(128)(4,1)S(1)}, s32[]{:S(2)}) async-start(s8[8388608]{0:T(1024)(128)(4,1)} %bitcast.124), calls=%async_computation.3 | async-start | bytes 8388608

commit v2 on v1

--- a/solution.py
+++ b/solution.py
@@ -35,9 +35,10 @@
     return (y_f32 + out_proj.astype(jnp.bfloat16).astype(jnp.float32)).astype(jnp.bfloat16)
 
 
-def combine_kernel(dims, route_ref, out_ref, resid_ref, y_ref,
-                   obuf, hbuf, routes, table, wterm, p1, p2, p3, r1, r2, r3, own, ysend, yland,
-                   o_loc, o_snd, o_rcv, h_loc, h_snd, h_rcv, t_loc, t_snd, t_rcv,
+def combine_kernel(dims, owner_ref, id_ref, slot_ref, gate_ref, out_ref, resid_ref, y_ref,
+                   obuf, hbuf, routes, ids, slots, gates, owners, goes, table, wterm,
+                   p1, p2, p3, r1, r2, r3, own, ysend, yland,
+                   o_loc, o_snd, o_rcv, h_loc, h_snd, h_rcv, t_loc, t_snd, t_rcv, w_snd, w_rcv, w_loc,
                    s1, s2, s3, q1, q2, q3, ys, yr):
     n_ep, n_st, n_loc, cap, slot_pad, seq_len, top_k, half = dims
     n_chip = n_ep // CORES
@@ -53,36 +54,43 @@
     side = [lax.rem(me + n_ep - CORES, n_ep), lax.rem(me + CORES, n_ep)]
     my_cols = pl.ds(pl.multiple_of(core * half, 128), half)
     sib_cols = pl.ds(pl.multiple_of((1 - core) * half, 128), half)
-
-    loc = []
-    for h in range(n_ep):
-        loc.append(pltpu.make_async_copy(out_ref.at[:, pl.ds(h * cap, cap), my_cols],
-                                         obuf.at[h, pl.ds(core * n_loc, n_loc), pl.ds(0, cap)], o_loc.at[h]))
-        loc[-1].start()
-    h_copy = pltpu.make_async_copy(resid_ref.at[:, my_cols], hbuf.at[core], h_loc)
-    h_copy.start()
-    t_copy = pltpu.make_async_copy(route_ref, routes.at[me], t_loc)
-    t_copy.start()
-
+    order = [q + n_half * ab for q in range(n_half) for ab in range(2)]
+
+    small = [pltpu.make_async_copy(src, dst, t_loc.at[i])
+             for i, (src, dst) in enumerate(((id_ref, ids), (slot_ref, slots), (gate_ref, gates)))]
+    for copy in small:
+        copy.start()
     barrier = pltpu.get_barrier_semaphore()
     for k in range(1, n_ep):
         pl.semaphore_signal(barrier, inc=1, device_id={'ep': lax.rem(me + k, n_ep)}, device_id_type=MESH)
     for other in (nxt, prv):
         for jc in range(CORES):
             pl.semaphore_signal(barrier, inc=1, device_id={'pp': other, 'ep': chip * CORES + jc}, device_id_type=MESH)
+    for h in order:
+        pltpu.make_async_copy(out_ref.at[:, pl.ds(h * cap, cap), my_cols],
+                              obuf.at[h, pl.ds(core * n_loc, n_loc), pl.ds(0, cap)], o_loc.at[h]).start()
+    h_copy = pltpu.make_async_copy(resid_ref.at[:, my_cols], hbuf.at[core], h_loc)
+    h_copy.start()
+    for copy in small:
+        copy.wait()
+    key = jnp.where(slots[...] >= 0, ids[...] * slot_pad + slots[...] - me * cap, -1)
+    routes[me, :top_k] = key.astype(jnp.float32).T
+    routes[me, top_k:] = gates[...].T
     if slot_pad > cap:
         for h in range(n_ep):
             obuf[h, :, cap:, :] = jnp.zeros((CORES * n_loc, slot_pad - cap, half), jnp.bfloat16)
     pl.semaphore_wait(barrier, n_ep - 1 + 2 * CORES)
 
+    w_out = pltpu.make_async_remote_copy(owner_ref, owners, w_snd, w_rcv, device_id={'pp': prv}, device_id_type=MESH)
+    w_out.start()
     t_out = []
-    for k in range(1, n_ep):
+    for k in (n_chip, n_chip - 1, n_chip + 1, 2, n_ep - 2, 1, n_ep - 1):
         peer = lax.rem(me + k, n_ep)
-        t_out.append(pltpu.make_async_remote_copy(route_ref, routes.at[me], t_snd.at[k - 1], t_rcv.at[me],
+        t_out.append(pltpu.make_async_remote_copy(routes.at[me], routes.at[me], t_snd.at[k - 1], t_rcv.at[me],
                                                   device_id={'ep': peer}, device_id_type=MESH))
         t_out[-1].start()
     o_out = []
-    for h in range(n_ep):
+    for h in order:
         o_out.append(pltpu.make_async_remote_copy(out_ref.at[:, pl.ds(h * cap, cap), sib_cols],
                                                   obuf.at[h, pl.ds(core * n_loc, n_loc), pl.ds(0, cap)],
                                                   o_snd.at[h], o_rcv.at[h],
@@ -92,13 +100,14 @@
                                          device_id={'ep': sib}, device_id_type=MESH)
     h_out.start()
 
-    t_copy.wait()
+    w_out.wait_recv()
+    goes_copy = pltpu.make_async_copy(owners, goes, w_loc)
+    goes_copy.start()
     for k in range(1, n_ep):
         src = lax.rem(me + k, n_ep)
-        pltpu.make_async_remote_copy(route_ref, routes.at[src], t_snd.at[k - 1], t_rcv.at[src],
+        pltpu.make_async_remote_copy(routes.at[src], routes.at[src], t_snd.at[k - 1], t_rcv.at[src],
                                      device_id={'ep': src}, device_id_type=MESH).wait_recv()
-    h_copy.wait()
-    h_out.wait_recv()
+    goes_copy.wait()
 
     def o_wait(h):
         pltpu.make_async_copy(out_ref.at[:, pl.ds(0, cap), my_cols],
@@ -115,7 +124,6 @@
 
     def partial(q, ab):
         h = q + n_half * ab
-        o_wait(h)
         rows = routes[h]
         rows = jnp.concatenate([rows, jnp.zeros((128 - rows.shape[0], tok_dev), jnp.float32)], axis=0)
         table[...] = rows.T
@@ -125,10 +133,21 @@
         for r in range(n_chip):
             for jc in range(CORES):
                 j = lax.rem(dest[r], n_chip) * CORES + jc
-                picks.append(pl.multiple_of(j * seq_len, seq_len))
+                pick = 0
+                for b in range(n_ep):
+                    seq = goes[0, j * n_ep + b] - h * n_ep
+                    pick = jnp.where(jnp.logical_and(seq >= 0, seq < n_ep), seq, pick)
+                picks.append(pick)
+
+        def chosen(pick, load):
+            got = load(0)
+            for s in range(1, n_ep):
+                got = jnp.where(pick == s, load(s), got)
+            return got
+
         base = (chip * depth).astype(jnp.float32)
-        for b, start in enumerate(picks):
-            rt = table[pl.ds(start, seq_len), :]
+        for b, pick in enumerate(picks):
+            rt = chosen(pick, lambda s: table[s * seq_len:(s + 1) * seq_len, :])
             w = jnp.zeros((seq_len, depth), jnp.float32)
             for j in range(top_k):
                 key = rt[:, j:j + 1] - base
@@ -141,12 +160,13 @@
                 wterm[pl.ds(t * tok_dev + b * seq_len, seq_len), :] = term
 
         dsts = [p1.at[ab, q], p2.at[1 - ab, q], p3.at[ab, q], own.at[ab, q]]
+        o_wait(h)
 
         @pl.loop(0, half // width)
         def _(n):
             cols = pl.ds(pl.multiple_of(n * width, width), width)
-            slots = obuf[h, :, :, cols].reshape(depth, width)
-            res = jnp.dot(wterm[...], slots, preferred_element_type=jnp.float32)
+            slots_in = obuf[h, :, :, cols].reshape(depth, width)
+            res = jnp.dot(wterm[...], slots_in, preferred_element_type=jnp.float32)
             res = res[:tok_dev] + (res[tok_dev:2 * tok_dev] + res[2 * tok_dev:])
             for r in range(n_chip):
                 dsts[r][:, cols] = res[r * block:(r + 1) * block]
@@ -154,10 +174,15 @@
         @pl.when(h // CORES == chip)
         def _():
             hc = lax.rem(h, CORES)
-            for b, start in enumerate(picks):
-                dst = dsts[b // CORES]
-                rs = slice((b % CORES) * seq_len, (b % CORES + 1) * seq_len)
-                dst[rs, :] = dst[rs, :] + hbuf[hc, pl.ds(start, seq_len), :].astype(jnp.float32)
+
+            @pl.loop(0, half // width)
+            def _(n):
+                cols = pl.ds(pl.multiple_of(n * width, width), width)
+                for b, pick in enumerate(picks):
+                    dst = dsts[b // CORES]
+                    rs = slice((b % CORES) * seq_len, (b % CORES + 1) * seq_len)
+                    held = chosen(pick, lambda s: hbuf[hc, s * seq_len:(s + 1) * seq_len, cols].astype(jnp.float32))
+                    dst[rs, cols] = dst[rs, cols] + held
 
     def ring(src, dst, snd, rcv, d, q):
         return pltpu.make_async_remote_copy(src.at[d, q], dst.at[d, q], snd.at[d, q], rcv.at[d, q],
@@ -168,6 +193,9 @@
                                             ys.at[q, jc], yr.at[core, q],
                                             device_id={'pp': nxt, 'ep': chip * CORES + jc}, device_id_type=MESH)
 
+    h_copy.wait()
+    h_out.wait_recv()
+
     @pl.loop(0, n_half + 2)
     def _(it):
         @pl.when(it < n_half)
@@ -175,18 +203,27 @@
             @pl.loop(0, 2)
             def _(ab):
                 partial(it, ab)
-            for d in range(2):
-                ring(p1, r1, s1, q1, d, it).start()
+                for d in range(2):
+                    @pl.when(ab == d)
+                    def _():
+                        ring(p1, r1, s1, q1, d, it).start()
+
+                        @pl.when(it == 0)
+                        def _():
+                            ring(p2, r2, s2, q2, 1 - d, it).start()
 
         @pl.when(jnp.logical_and(it >= 1, it <= n_half))
         def _():
             q = it - 1
-            for d in range(2):
-                ring(p2, r2, s2, q2, d, q).start()
             for d in range(2):
                 ring(p1, r1, s1, q1, d, q).wait_recv()
                 p3[d, q] = p3[d, q] + r1[d, q]
                 ring(p3, r3, s3, q3, d, q).start()
+
+        @pl.when(jnp.logical_and(it >= 1, it < n_half))
+        def _():
+            for d in range(2):
+                ring(p2, r2, s2, q2, d, it).start()
 
         @pl.when(it >= 2)
         def _():
@@ -211,10 +248,9 @@
                                          device_id={'pp': nxt, 'ep': me}, device_id_type=MESH).wait_recv()
     y_ref[...] = yland[...]
 
-    for k in range(1, n_ep):
-        t_out[k - 1].wait_send()
-    for h in range(n_ep):
-        o_out[h].wait_send()
+    w_out.wait_send()
+    for copy in t_out + o_out:
+        copy.wait_send()
     h_out.wait_send()
 
     @pl.loop(0, n_half)
@@ -230,7 +266,6 @@
 def solution(mesh):
     n_stages = mesh.shape['pp']
     n_ep = mesh.shape['ep']
-    prev_rank = [((src_rank + 1) % n_stages, src_rank) for src_rank in range(n_stages)]
     group_axes = ('data', 'pp')
 
     def device_step(expert_out, expert_id, slot_id, gate, resid, owner, norm_w, w_q, w_k, w_v, w_o):
@@ -246,19 +281,6 @@
         n_half = n_ep // 2
         block = CORES * seq_len
 
-        grid = owner[0].reshape(n_ep, seq_dev)
-        homes = jnp.arange(n_ep)[:, None, None]
-        pick = jnp.sum(jnp.where(grid[None] // seq_dev == homes, grid[None] - homes * seq_dev, 0), axis=2)
-        pick = lax.ppermute(pick.reshape(-1).astype(jnp.int32), 'pp', prev_rank)
-        my_src = lax.dynamic_index_in_dim(grid // seq_dev, dev_index, 0, keepdims=False)
-        pos = (my_src % n_half * 2 + my_src // n_half).astype(jnp.int32)
-
-        key = jnp.where(slot_id[0, 0] >= 0, expert_id[0, 0] * slot_pad + slot_id[0, 0] - dev_index * cap, -1)
-        leaving = lax.dynamic_index_in_dim(pick.reshape(n_ep, n_ep), dev_index, 0, keepdims=False)
-        route = jnp.concatenate([key.astype(jnp.float32), gate[0, 0]], axis=1)
-        route = jnp.take(route.reshape(seq_dev, seq_len, 2 * top_k), leaving, axis=0).reshape(tok_dev, 2 * top_k).T
-        held = jnp.take(resid[0, 0].reshape(seq_dev, seq_len, model_dim), leaving, axis=0).reshape(tok_dev, model_dim)
-
         dims = (n_ep, n_stages, n_loc, cap, slot_pad, seq_len, top_k, half)
         f32, bf16 = jnp.float32, jnp.bfloat16
         ringbuf = pltpu.VMEM((2, n_half, block, half), f32)
@@ -266,12 +288,17 @@
         y_owned = pl.pallas_call(
             functools.partial(combine_kernel, dims),
             out_shape=jax.ShapeDtypeStruct((n_ep, seq_len, model_dim), bf16),
-            in_specs=[pl.BlockSpec(memory_space=pltpu.VMEM)] + [pl.BlockSpec(memory_space=pl.ANY)] * 2,
+            in_specs=[pl.BlockSpec(memory_space=pl.ANY)] * 6,
             out_specs=pl.BlockSpec(memory_space=pltpu.VMEM),
             scratch_shapes=[
                 pltpu.VMEM((n_ep, CORES * n_loc, slot_pad, half), bf16),
                 pltpu.VMEM((CORES, tok_dev, half), bf16),
                 pltpu.VMEM((n_ep, 2 * top_k, tok_dev), f32),
+                pltpu.VMEM((tok_dev, top_k), jnp.int32),
+                pltpu.VMEM((tok_dev, top_k), jnp.int32),
+                pltpu.VMEM((tok_dev, top_k), f32),
+                pltpu.VMEM((1, n_ep * seq_dev), jnp.int32),
+                pltpu.SMEM((1, n_ep * seq_dev), jnp.int32),
                 pltpu.VMEM((tok_dev, 128), f32),
                 pltpu.VMEM((3 * tok_dev, CORES * n_loc * slot_pad), bf16),
                 ringbuf, ringbuf, ringbuf, ringbuf, ringbuf, ringbuf, ringbuf,
@@ -279,15 +306,17 @@
                 pltpu.VMEM((n_ep, seq_len, model_dim), bf16),
                 dma((n_ep,)), dma((n_ep,)), dma((n_ep,)),
                 dma, dma, dma,
-                dma, dma((n_ep - 1,)), dma((n_ep,)),
+                dma((3,)), dma((n_ep - 1,)), dma((n_ep,)),
+                dma, dma, dma,
                 dma((2, n_half)), dma((2, n_half)), dma((2, n_half)),
                 dma((2, n_half)), dma((2, n_half)), dma((2, n_half)),
                 dma((n_half, CORES)), dma((CORES, n_half)),
             ],
             compiler_params=pltpu.CompilerParams(collective_id=0, has_side_effects=True, vmem_limit_bytes=60 * 2 ** 20),
             name='combine',
-        )(route, expert_out[0, 0], held)
-        y_owned = jnp.take(y_owned, pos, axis=0)
+        )(owner, expert_id[0, 0], slot_id[0, 0], gate[0, 0], expert_out[0, 0], resid[0, 0])
+        source = lax.dynamic_slice_in_dim(owner[0], dev_index * seq_dev, seq_dev) // seq_dev
+        y_owned = jnp.take(y_owned, source % n_half * 2 + source // n_half, axis=0)
         z_owned = attend_local(y_owned[None], norm_w[0], w_q[0], w_k[0], w_v[0], w_o[0])
         return z_owned.reshape(1, tok_dev, model_dim)[None]
 

time: 141 us -> 135 us (0.957)
  starting transfers between devices: 5.22 us -> 0 us
  other arithmetic: 4.59 us -> 1.94 us
  matrix products: 24.6 us -> 27.2 us
  Pallas kernels: 101 us -> 99.4 us
    ppermute x1 -> x0, starting transfers between devices: 5.22 us -> none  [device_step(): pick = lax.ppermute(pick.reshape(-1).astype(jnp.int32), 'pp', prev_rank)]
    dot_general x3, matrix products: 12.9 us -> 17.2 us  [project(): jnp.einsum('msld,de->msle', normed, weight, preferred_element_type=jnp.fl...]
    unnamed x13 -> x9, local copies, waits for them, and re-layouts: 0.55 us -> 4.46 us
    pallas_call x1, Pallas kernels: 101 us -> 99.4 us  [device_step(): pl.pallas_call(functools.partial(combine_kernel, dims), out_shape=jax.Sha...]
    gather x5 -> x1, local copies, waits for them, and re-layouts: 3.12 us -> 1.84 us  [device_step(): y_owned = jnp.take(y_owned, source % n_half * 2 + source // n_half, axis=0)]
  transfers between devices with their start and end apart: 1 -> 0, of which waited for: 0 -> 0; matrix products, arithmetic and copies ran while one was open for 1% -> 0% of each run, Pallas kernels for 0% -> 0%
where the time goes in v2:
time: 135 us
  Pallas kernels  99.4 us (74%)
  matrix products  27.2 us (20%)
  local copies, waits for them, and re-layouts  6.3 us (5%)
  other arithmetic  1.94 us (1%)
    pallas_call x1, Pallas kernels, device_step(): pl.pallas_call(functools.partial(combine_kernel, dims), out_shape=jax.Sha...  99.4 us
    dot_general x3, matrix products, project(): jnp.einsum('msld,de->msle', normed, weight, preferred_element_type=jnp.fl...  17.2 us
    dot_general x1, matrix products, attend_local(): jnp.einsum('msqhe,hed->msqd', head_mix, w_o.reshape(n_heads, HEAD_DIM, mo...  7.49 us
    unnamed x9, local copies, waits for them, and re-layouts  4.46 us

profile of v2, /device:TPU:97, one launch (start us, length us, event | category | flops | bytes accessed | tf_op | source)
XLA Modules:
  0.0 135.0 jit_solution(2609811504139558856)
XLA Ops:
  0.0 0.7 compare_and_fusion
  0.7 0.8 fusion.54
  1.5 1.5 %copy.12 = s32[1,1,256,8]{3,2,1,0:T(8,128)} copy(s32[1,1,256,8]{2,3,1,0:T(8,128)} %param.12) | data formatting | bytes 16384 | tf_op args[1]
  3.0 1.5 %copy.13 = s32[1,1,256,8]{3,2,1,0:T(8,128)} copy(s32[1,1,256,8]{2,3,1,0:T(8,128)} %param.13) | data formatting | bytes 16384 | tf_op args[2]
  4.5 1.5 %copy.14 = f32[1,1,256,8]{3,2,1,0:T(8,128)} copy(f32[1,1,256,8]{2,3,1,0:T(8,128)} %param.14) | data formatting | bytes 16384 | tf_op args[3]
  6.0 99.4 %combine.1 = bf16[8,32,2048]{2,1,0:T(8,128)(2,1)} custom-call(s32[1,64]{1,0:T(1,128)} %owner_ref.1, s32[256,8]{1,0:T(8,128)} %bitcast.110, s32[256,8]{1,0:T(8,128)} %bitcast.111, f32[256,8]{1,0:T(8,128)} %bitcast.112, bf16[8,320,2048]{2,1,0:T(8,128)(2,1)} %bitcast.108, bf16[256,2048]{1,0:T(8,128)(2,1)} %bitcast.109), custom_call_target="tpu_custom_call" | custom-call | tf_op jit(solution)/shard_map/combine/pallas_call | solution.py:288
  105.4 0.0 copy-start
  105.4 1.8 %gather_fusion = bf16[8,32,2048]{2,1,0:T(8,128)(2,1)S(1)} fusion(bf16[8,32,2048]{2,1,0:T(8,128)(2,1)} %combine.1, s32[1024]{0:T(1024)S(1)} %pad_clamp_fusion), kind=kCustom, calls=%fused_computation | custom fusion | bytes 2097184 | tf_op jit(solution)/shard_map/jit(_take)/gather | solution.py:319
  107.3 0.0 slice-start
  107.3 0.4 fusion.19
  107.7 0.0 copy-done
  107.7 0.0 slice-start.1
  107.7 7.0 %fusion.27 = bf16[8,4,16,8,128]{4,3,2,1,0:T(8,128)(2,1)} fusion(bf16[1,2048,2048]{2,1,0:T(8,128)(2,1)} %param.18, f32[2048]{0:T(1024)S(1)} %bitcast.116, f32[8,32]{1,0:T(8,128)S(1)} %add_rsqrt_fusion, bf16[8,32,2048]{2,1,0:T(8,128)(2,1)S(1)} %gather_fusion, pred[8]{0:T(512)(128)(4,1)S(1)} %compare_and_fusion), kind=kOutput, calls=%fused_computation.28 | convolution fusion | flops 2150629376 | bytes 10494984 | tf_op jit(solution)/shard_map/msld,de->msle/dot_general | solution.py:24
  114.8 0.0 slice-done
  114.8 0.0 slice-done.1
  114.8 3.4 %fusion.24 = bf16[8,4,16,8,128]{4,3,2,1,0:T(8,128)(2,1)} fusion(bf16[1,2048,2048]{2,1,0:T(8,128)(2,1)S(1)} %bitcast.114, f32[2048]{0:T(1024)S(1)} %bitcast.117, f32[8,32]{1,0:T(8,128)S(1)} %add_rsqrt_fusion, bf16[8,32,2048]{2,1,0:T(8,128)(2,1)S(1)} %gather_fusion, pred[8]{0:T(512)(128)(4,1)S(1)} %compare_and_fusion), kind=kOutput, calls=%fused_computation.27 | convolution fusion | flops 2150629376 | bytes 10494984 | tf_op jit(solution)/shard_map/msld,de->msle/dot_general | solution.py:24
  118.2 2.5 %fusion.69 = (f32[8,16,32]{2,1,0:T(8,128)S(1)}, f32[8,16,32,32]{2,3,1,0:T(8,128)S(1)}) fusion(pred[32,32]{0,1:T(8,128)(4,1)S(1)} %iota_compare_fusion, bf16[8,4,16,8,128]{4,3,2,1,0:T(8,128)(2,1)} %fusion.24, bf16[8,4,16,8,128]{4,3,2,1,0:T(8,128)(2,1)} %fusion.27), kind=kOutput, calls=%fused_computation.76 | convolution fusion | flops 34078752 | bytes 2638848 | tf_op jit(solution)/shard_map/sub | solution.py:32
  120.7 6.8 %fusion.30 = bf16[8,4,16,8,128]{4,3,2,1,0:T(8,128)(2,1)} fusion(bf16[1,2048,2048]{2,1,0:T(8,128)(2,1)} %param.20, f32[2048]{0:T(1024)S(1)} %bitcast.118, f32[8,32]{1,0:T(8,128)S(1)} %add_rsqrt_fusion, bf16[8,32,2048]{2,1,0:T(8,128)(2,1)S(1)} %gather_fusion, pred[8]{0:T(512)(128)(4,1)S(1)} %compare_and_fusion), kind=kOutput, calls=%fused_computation.29 | convolution fusion | flops 2150629376 | bytes 10494984 | tf_op jit(solution)/shard_map/msld,de->msle/dot_general | solution.py:24
  127.5 7.5 %fusion.9 = bf16[8,32,2048]{2,1,0:T(8,128)(2,1)} fusion(bf16[16,128,2048,1]{2,1,0,3:T(8,128)(2,1)} %bitcast.115, f32[8,16,32,32]{2,3,1,0:T(8,128)S(1)} %get-tuple-element.6, bf16[8,4,16,8,128]{4,3,2,1,0:T(8,128)(2,1)} %fusion.30, f32[8,16,32]{2,1,0:T(8,128)S(1)} %get-tuple-element.5, bf16[8,32,2048]{2,1,0:T(8,128)(2,1)S(1)} %gather_fusion, ...), kind=kOutput, calls=%fused_computation.14 | convolution fusion | flops 2184970240 | bytes 12075016 | tf_op jit(solution)/shard_map/msqhe,hed->msqd/dot_general | solution.py:34
  (4 shorter events, 0.0 us)
Async XLA Ops:
  105.4 2.3 %copy-start = (f32[1,2048]{1,0:T(1,128)S(1)}, f32[1,2048]{1,0:T(1,128)}, u32[]{:S(2)}) copy-start(f32[1,2048]{1,0:T(1,128)} %param.17) | copy-start | bytes 24580
  107.3 7.5 %slice-start = ((s8[8388608]{0:T(1024)(128)(4,1)}), s8[4194304]{0:T(1024)(128)(4,1)S(1)}, s32[]{:S(2)}) async-start(s8[8388608]{0:T(1024)(128)(4,1)} %bitcast.113), calls=%async_computation | async-start | bytes 8388608
  107.7 7.0 %slice-start.1 = ((s8[8388608]{0:T(1024)(128)(4,1)}), s8[4194304]{0:T(1024)(128)(4,1)S(1)}, s32[]{:S(2)}) async-start(s8[8388608]{0:T(1024)(128)(4,1)} %bitcast.113), calls=%async_computation.1 | async-start | bytes 8388608

commit v3 on v2

--- a/solution.py
+++ b/solution.py
@@ -13,33 +13,11 @@
 CORES = 2
 
 
-def attend_local(y_owned, norm_scale, w_q, w_k, w_v, w_o):
-    n_micro, n_seqs, seq_len, model_dim = y_owned.shape
-    n_heads = w_q.shape[1] // HEAD_DIM
-    y_f32 = y_owned.astype(jnp.float32)
-    inv_rms = lax.rsqrt(jnp.mean(y_f32 * y_f32, axis=-1, keepdims=True) + NORM_EPS)
-    normed = (y_f32 * inv_rms * norm_scale).astype(jnp.bfloat16)
-
-    def project(weight):
-        proj_out = jnp.einsum('msld,de->msle', normed, weight, preferred_element_type=jnp.float32)
-        return proj_out.astype(jnp.bfloat16).reshape(n_micro, n_seqs, seq_len, n_heads, HEAD_DIM)
-
-    queries = project(w_q)
-    key_vecs = project(w_k)
-    values = project(w_v)
-    scores = jnp.einsum('msqhe,mskhe->mshqk', queries, key_vecs, preferred_element_type=jnp.float32) * (HEAD_DIM ** -0.5)
-    causal = jnp.arange(seq_len)[:, None] >= jnp.arange(seq_len)[None, :]
-    attn_probs = jax.nn.softmax(jnp.where(causal, scores, -1e30), axis=-1).astype(jnp.bfloat16)
-    head_mix = jnp.einsum('mshqk,mskhe->msqhe', attn_probs, values, preferred_element_type=jnp.float32).astype(jnp.bfloat16)
-    out_proj = jnp.einsum('msqhe,hed->msqd', head_mix, w_o.reshape(n_heads, HEAD_DIM, model_dim), preferred_element_type=jnp.float32)
-    return (y_f32 + out_proj.astype(jnp.bfloat16).astype(jnp.float32)).astype(jnp.bfloat16)
-
-
-def combine_kernel(dims, owner_ref, id_ref, slot_ref, gate_ref, out_ref, resid_ref, y_ref,
+def stage_kernel(dims, owner_ref, id_ref, slot_ref, gate_ref, out_ref, resid_ref, norm_ref, q_ref, k_ref, v_ref, o_ref, z_ref,
                    obuf, hbuf, routes, ids, slots, gates, owners, goes, table, wterm,
-                   p1, p2, p3, r1, r2, r3, own, ysend, yland,
+                   p1, p2, p3, r1, r2, r3, own, ysend, yland, norm, wq, wk, wv, wo, xs, mix,
                    o_loc, o_snd, o_rcv, h_loc, h_snd, h_rcv, t_loc, t_snd, t_rcv, w_snd, w_rcv, w_loc,
-                   s1, s2, s3, q1, q2, q3, ys, yr):
+                   s1, s2, s3, q1, q2, q3, ys, yr, wt, zs):
     n_ep, n_st, n_loc, cap, slot_pad, seq_len, top_k, half = dims
     n_chip = n_ep // CORES
     n_half = n_ep // 2
@@ -74,8 +52,8 @@
     for copy in small:
         copy.wait()
     key = jnp.where(slots[...] >= 0, ids[...] * slot_pad + slots[...] - me * cap, -1)
-    routes[me, :top_k] = key.astype(jnp.float32).T
-    routes[me, top_k:] = gates[...].T
+    routes[me, :top_k] = key.astype(jnp.float32)
+    routes[me, top_k:] = gates[...]
     if slot_pad > cap:
         for h in range(n_ep):
             obuf[h, :, cap:, :] = jnp.zeros((CORES * n_loc, slot_pad - cap, half), jnp.bfloat16)
@@ -119,6 +97,11 @@
 
     depth = CORES * n_loc * slot_pad
     width = min(256, half)
+    n_sub = half // width
+    model = CORES * half
+    tile = min(512, model)
+    weights = [pltpu.make_async_copy(src, dst, wt.at[i])
+               for i, (src, dst) in enumerate(((q_ref, wq), (k_ref, wk), (v_ref, wv), (o_ref, wo), (norm_ref, norm)))]
     lane = lax.broadcasted_iota(jnp.int32, (seq_len, depth), 1).astype(jnp.float32)
     block = CORES * seq_len
 
@@ -159,7 +142,7 @@
             for t, term in enumerate((hi, mid, low)):
                 wterm[pl.ds(t * tok_dev + b * seq_len, seq_len), :] = term
 
-        dsts = [p1.at[ab, q], p2.at[1 - ab, q], p3.at[ab, q], own.at[ab, q]]
+        dsts = [p1.at[ab, q], p2.at[1 - ab, q], p3.at[ab, lax.rem(q, 2)], own.at[ab, lax.rem(q, 3)]]
         o_wait(h)
 
         @pl.loop(0, half // width)
@@ -188,15 +171,78 @@
         return pltpu.make_async_remote_copy(src.at[d, q], dst.at[d, q], snd.at[d, q], rcv.at[d, q],
                                             device_id={'ep': side[d]}, device_id_type=MESH)
 
-    def hop(q, jc):
-        return pltpu.make_async_remote_copy(ysend.at[q, jc], yland.at[pl.ds(2 * q, 2), :, my_cols],
-                                            ys.at[q, jc], yr.at[core, q],
-                                            device_id={'pp': nxt, 'ep': chip * CORES + jc}, device_id_type=MESH)
+    def sub(n):
+        return pl.ds(pl.multiple_of(n * width, width), width)
+
+    def last_leg(d, q, n):
+        return pltpu.make_async_remote_copy(r1.at[d, q, :, sub(n)], r3.at[d, q, :, sub(n)], s3.at[d, q, n], q3.at[d, q, n],
+                                            device_id={'ep': side[d]}, device_id_type=MESH)
+
+    def hop(q, jc, n, c, to):
+        cols = pl.ds(pl.multiple_of(c * half + n * width, width), width)
+        return pltpu.make_async_remote_copy(ysend.at[q, jc, :, :, sub(n)], yland.at[pl.ds(2 * q, 2), :, cols],
+                                            ys.at[q, jc, n], yr.at[c, q, n],
+                                            device_id={'pp': nxt, 'ep': to}, device_id_type=MESH)
+
+    def finish(q, n):
+        @pl.when(n == 0)
+        def _():
+            for d in range(2):
+                ring(p2, r2, s2, q2, d, q).wait_recv()
+        cols = sub(n)
+        for d in range(2):
+            last_leg(d, q, n).wait_recv()
+        for ab in range(2):
+            total = own[ab, lax.rem(q, 3), :, cols] + (r3[ab, q, :, cols] + r2[1 - ab, q, :, cols])
+            rounded = total.astype(jnp.bfloat16)
+            for jc in range(CORES):
+                ysend[q, jc, ab, :, cols] = rounded[jc * seq_len:(jc + 1) * seq_len]
+        for jc in range(CORES):
+            hop(q, jc, n, core, chip * CORES + jc).start()
+
+    n_tok = 2 * seq_len
+    row = lax.broadcasted_iota(jnp.int32, (n_tok, n_tok), 0)
+    col = lax.broadcasted_iota(jnp.int32, (n_tok, n_tok), 1)
+    causal = jnp.logical_and(row >= col, row // seq_len == col // seq_len)
+
+    def normalise(q):
+        for c in range(CORES):
+            for n in range(n_sub):
+                hop(q, 0, n, c, me).wait_recv()
+        for ab in range(2):
+            y = yland[2 * q + ab].astype(jnp.float32)
+            inv = lax.rsqrt(jnp.mean(y * y, axis=-1, keepdims=True) + NORM_EPS)
+            xs[ab * seq_len:(ab + 1) * seq_len, :] = (y * inv * norm[...]).astype(jnp.bfloat16)
+
+    def attend(n):
+        cols = pl.ds(pl.multiple_of(n * tile, tile), tile)
+        x = xs[...]
+        qt, kt, vt = (jnp.dot(x, w[:, cols], preferred_element_type=jnp.float32).astype(jnp.bfloat16) for w in (wq, wk, wv))
+        for hd in range(tile // HEAD_DIM):
+            hs = slice(hd * HEAD_DIM, (hd + 1) * HEAD_DIM)
+            scores = lax.dot_general(qt[:, hs], kt[:, hs], (((1,), (1,)), ((), ())), preferred_element_type=jnp.float32)
+            scores = jnp.where(causal, scores * (HEAD_DIM ** -0.5), -1e30)
+            raised = jnp.exp(scores - jnp.max(scores, axis=-1, keepdims=True))
+            probs = (raised / jnp.sum(raised, axis=-1, keepdims=True)).astype(jnp.bfloat16)
+            mixed = jnp.dot(probs, vt[:, hs], preferred_element_type=jnp.float32).astype(jnp.bfloat16)
+            mix[:, pl.ds(pl.multiple_of(n * tile + hd * HEAD_DIM, HEAD_DIM), HEAD_DIM)] = mixed
+
+    def project(q):
+        @pl.loop(0, model // tile)
+        def _(n):
+            cols = pl.ds(pl.multiple_of(n * tile, tile), tile)
+            out = jnp.dot(mix[...], wo[:, cols], preferred_element_type=jnp.float32).astype(jnp.bfloat16).astype(jnp.float32)
+            for ab in range(2):
+                y = yland[2 * q + ab, :, cols].astype(jnp.float32)
+                yland[2 * q + ab, :, cols] = (y + out[ab * seq_len:(ab + 1) * seq_len]).astype(jnp.bfloat16)
+
+    def store(q):
+        return pltpu.make_async_copy(yland.at[pl.ds(2 * q, 2)], z_ref.at[pl.ds(2 * q, 2)], zs.at[q])
 
     h_copy.wait()
     h_out.wait_recv()
 
-    @pl.loop(0, n_half + 2)
+    @pl.loop(0, n_half + 3)
     def _(it):
         @pl.when(it < n_half)
         def _():
@@ -212,41 +258,48 @@
                         def _():
                             ring(p2, r2, s2, q2, 1 - d, it).start()
 
+        @pl.when(it == 0)
+        def _():
+            for copy in weights:
+                copy.start()
+
         @pl.when(jnp.logical_and(it >= 1, it <= n_half))
         def _():
             q = it - 1
             for d in range(2):
                 ring(p1, r1, s1, q1, d, q).wait_recv()
-                p3[d, q] = p3[d, q] + r1[d, q]
-                ring(p3, r3, s3, q3, d, q).start()
+                r1[d, q] = p3[d, lax.rem(q, 2)] + r1[d, q]
+                for n in range(n_sub):
+                    last_leg(d, q, n).start()
 
         @pl.when(jnp.logical_and(it >= 1, it < n_half))
         def _():
             for d in range(2):
                 ring(p2, r2, s2, q2, d, it).start()
 
-        @pl.when(it >= 2)
-        def _():
-            q = it - 2
-            for d in range(2):
-                ring(p2, r2, s2, q2, d, q).wait_recv()
-                ring(p3, r3, s3, q3, d, q).wait_recv()
-            for ab in range(2):
-                total = own[ab, q] + (r3[ab, q] + r2[1 - ab, q])
-                rounded = total.astype(jnp.bfloat16)
-                for jc in range(CORES):
-                    ysend[q, jc, ab] = rounded[jc * seq_len:(jc + 1) * seq_len]
-            for jc in range(CORES):
-                hop(q, jc).start()
-
-    @pl.loop(0, n_half)
-    def _(q):
-        for c in range(CORES):
-            cols = pl.ds(c * half, half)
-            pltpu.make_async_remote_copy(ysend.at[q, 0], yland.at[pl.ds(2 * q, 2), :, cols],
-                                         ys.at[q, 0], yr.at[c, q],
-                                         device_id={'pp': nxt, 'ep': me}, device_id_type=MESH).wait_recv()
-    y_ref[...] = yland[...]
+        @pl.when(it == 3)
+        def _():
+            for copy in weights:
+                copy.wait()
+
+        @pl.when(it >= 3)
+        def _():
+            normalise(it - 3)
+
+        @pl.loop(0, n_sub)
+        def _(n):
+            @pl.when(it >= 3)
+            def _():
+                attend(n)
+
+            @pl.when(jnp.logical_and(it >= 2, it < n_half + 2))
+            def _():
+                finish(it - 2, n)
+
+        @pl.when(it >= 3)
+        def _():
+            project(it - 3)
+            store(it - 3).start()
 
     w_out.wait_send()
     for copy in t_out + o_out:
@@ -258,9 +311,12 @@
         for d in range(2):
             ring(p1, r1, s1, q1, d, q).wait_send()
             ring(p2, r2, s2, q2, d, q).wait_send()
-            ring(p3, r3, s3, q3, d, q).wait_send()
+            for n in range(n_sub):
+                last_leg(d, q, n).wait_send()
         for jc in range(CORES):
-            hop(q, jc).wait_send()
+            for n in range(n_sub):
+                hop(q, jc, n, core, chip * CORES + jc).wait_send()
+        store(q).wait()
 
 
 def solution(mesh):
@@ -283,42 +339,52 @@
 
         dims = (n_ep, n_stages, n_loc, cap, slot_pad, seq_len, top_k, half)
         f32, bf16 = jnp.float32, jnp.bfloat16
-        ringbuf = pltpu.VMEM((2, n_half, block, half), f32)
+        n_sub = half // min(256, half)
+        assert model_dim // min(512, model_dim) == n_sub and n_half > 3
+
+        def ringbuf(slots):
+            return pltpu.VMEM((2, slots, block, half), f32)
+
+        square = pltpu.VMEM((model_dim, model_dim), bf16)
         dma = pltpu.SemaphoreType.DMA
-        y_owned = pl.pallas_call(
-            functools.partial(combine_kernel, dims),
+        z_pairs = pl.pallas_call(
+            functools.partial(stage_kernel, dims),
             out_shape=jax.ShapeDtypeStruct((n_ep, seq_len, model_dim), bf16),
-            in_specs=[pl.BlockSpec(memory_space=pl.ANY)] * 6,
-            out_specs=pl.BlockSpec(memory_space=pltpu.VMEM),
+            in_specs=[pl.BlockSpec(memory_space=pl.ANY)] * 11,
+            out_specs=pl.BlockSpec(memory_space=pl.ANY),
             scratch_shapes=[
                 pltpu.VMEM((n_ep, CORES * n_loc, slot_pad, half), bf16),
                 pltpu.VMEM((CORES, tok_dev, half), bf16),
                 pltpu.VMEM((n_ep, 2 * top_k, tok_dev), f32),
-                pltpu.VMEM((tok_dev, top_k), jnp.int32),
-                pltpu.VMEM((tok_dev, top_k), jnp.int32),
-                pltpu.VMEM((tok_dev, top_k), f32),
+                pltpu.VMEM((top_k, tok_dev), jnp.int32),
+                pltpu.VMEM((top_k, tok_dev), jnp.int32),
+                pltpu.VMEM((top_k, tok_dev), f32),
                 pltpu.VMEM((1, n_ep * seq_dev), jnp.int32),
                 pltpu.SMEM((1, n_ep * seq_dev), jnp.int32),
                 pltpu.VMEM((tok_dev, 128), f32),
                 pltpu.VMEM((3 * tok_dev, CORES * n_loc * slot_pad), bf16),
-                ringbuf, ringbuf, ringbuf, ringbuf, ringbuf, ringbuf, ringbuf,
+                ringbuf(n_half), ringbuf(n_half), ringbuf(2), ringbuf(n_half), ringbuf(n_half), ringbuf(n_half), ringbuf(3),
                 pltpu.VMEM((n_half, CORES, 2, seq_len, half), bf16),
                 pltpu.VMEM((n_ep, seq_len, model_dim), bf16),
+                pltpu.VMEM((1, model_dim), f32),
+                square, square, square, square,
+                pltpu.VMEM((2 * seq_len, model_dim), bf16),
+                pltpu.VMEM((2 * seq_len, model_dim), bf16),
                 dma((n_ep,)), dma((n_ep,)), dma((n_ep,)),
                 dma, dma, dma,
                 dma((3,)), dma((n_ep - 1,)), dma((n_ep,)),
                 dma, dma, dma,
-                dma((2, n_half)), dma((2, n_half)), dma((2, n_half)),
-                dma((2, n_half)), dma((2, n_half)), dma((2, n_half)),
-                dma((n_half, CORES)), dma((CORES, n_half)),
+                dma((2, n_half)), dma((2, n_half)), dma((2, n_half, n_sub)),
+                dma((2, n_half)), dma((2, n_half)), dma((2, n_half, n_sub)),
+                dma((n_half, CORES, n_sub)), dma((CORES, n_half, n_sub)), dma((5,)), dma((n_half,)),
             ],
-            compiler_params=pltpu.CompilerParams(collective_id=0, has_side_effects=True, vmem_limit_bytes=60 * 2 ** 20),
-            name='combine',
-        )(owner, expert_id[0, 0], slot_id[0, 0], gate[0, 0], expert_out[0, 0], resid[0, 0])
+            compiler_params=pltpu.CompilerParams(collective_id=0, has_side_effects=True, vmem_limit_bytes=67043328),
+            name='stage',
+        )(owner, expert_id[0, 0].T, slot_id[0, 0].T, gate[0, 0].T, expert_out[0, 0], resid[0, 0],
+          norm_w, w_q[0], w_k[0], w_v[0], w_o[0])
         source = lax.dynamic_slice_in_dim(owner[0], dev_index * seq_dev, seq_dev) // seq_dev
-        y_owned = jnp.take(y_owned, source % n_half * 2 + source // n_half, axis=0)
-        z_owned = attend_local(y_owned[None], norm_w[0], w_q[0], w_k[0], w_v[0], w_o[0])
-        return z_owned.reshape(1, tok_dev, model_dim)[None]
+        z_owned = jnp.take(z_pairs, source % n_half * 2 + source // n_half, axis=0)
+        return z_owned.reshape(1, 1, tok_dev, model_dim)
 
     tok_spec = P(group_axes, None, 'ep', None)
     weight_spec = P('pp', None, None)

time: 135 us -> 118 us (0.87)
  matrix products: 27.2 us -> 0 us
  Pallas kernels: 99.4 us -> 111 us
  local copies, waits for them, and re-layouts: 6.3 us -> 2.71 us
  other arithmetic: 1.94 us -> 3.9 us
    dot_general x4 -> x0, matrix products: 24.7 us -> none  [the longest x3 17.2 us: project(): jnp.einsum('msld,de->msle', normed, weight, preferred_element_type=jnp.fl...]
    pallas_call x1, Pallas kernels: 99.4 us -> 111 us  [device_step(): pl.pallas_call(functools.partial(stage_kernel, dims), out_shape=jax.Shape...]
    unnamed x9 -> x0, local copies, waits for them, and re-layouts: 4.46 us -> none
    sub x1 -> x0, matrix products: 2.51 us -> none  [attend_local(): jax.nn.softmax(jnp.where(causal, scores, -1e+30), axis=-1)]
    select_n x1 -> x2, other arithmetic: 0.75 us -> 2.55 us  [device_step(): z_owned = jnp.take(z_pairs, source % n_half * 2 + source // n_half, axis=0)]
where the time goes in v3:
time: 118 us; the launch traced here: 117 us
  Pallas kernels  111 us (94%)
  other arithmetic  3.9 us (3%)
  local copies, waits for them, and re-layouts  2.71 us (2%)
    pallas_call x1, Pallas kernels, device_step(): pl.pallas_call(functools.partial(stage_kernel, dims), out_shape=jax.Shape...  111 us
    select_n x2, other arithmetic, device_step(): z_owned = jnp.take(z_pairs, source % n_half * 2 + source // n_half, axis=0)  2.55 us

profile of v3, /device:TPU:97, one launch (start us, length us, event | category | flops | bytes accessed | tf_op | source)
XLA Modules:
  0.0 117.4 jit_solution(10245569200349565345)
XLA Ops:
  0.0 0.7 fusion.4
  0.7 0.8 compare_and_fusion
  1.5 0.1 broadcast_in_dim.14
  1.6 0.7 broadcast_in_dim.15
  2.3 0.6 pad_clamp_fusion
  2.9 110.8 %stage.1 = bf16[8,32,2048]{2,1,0:T(8,128)(2,1)} custom-call(s32[1,64]{1,0:T(1,128)} %owner_ref.1, s32[8,256]{1,0:T(8,128)} %bitcast.45, s32[8,256]{1,0:T(8,128)} %bitcast.46, f32[8,256]{1,0:T(8,128)} %bitcast.47, bf16[8,320,2048]{2,1,0:T(8,128)(2,1)} %bitcast.38, bf16[256,2048]{1,0:T(8,128)(2,1)} %bitcast.44, f32[1,2048]{1,0:T(1,128)} %norm_ref.1, ...), custom_call_target="tpu_custom_call" | custom-call | tf_op jit(solution)/shard_map/stage/pallas_call | solution.py:350
  113.6 2.0 %gather_fusion = bf16[8,32,2048]{2,1,0:T(8,128)(2,1)S(1)} fusion(bf16[8,32,2048]{2,1,0:T(8,128)(2,1)} %stage.1, s32[1024]{0:T(1024)} %pad_clamp_fusion), kind=kCustom, calls=%fused_computation | custom fusion | bytes 2097184 | tf_op jit(solution)/shard_map/jit(_take)/gather | solution.py:386
  115.6 1.8 %broadcast_select_fusion = bf16[1,1,256,2048]{3,2,1,0:T(8,128)(2,1)} fusion(bf16[1,1,256,2048]{3,2,1,0:T(8,128)(2,1)S(1)} %bitcast.43, pred[256]{0:T(512)(128)(4,1)} %broadcast_in_dim.15), kind=kLoop, calls=%fused_computation.1 | loop fusion | flops 524288 | bytes 2097408 | tf_op jit(solution)/shard_map/jit(_take)/select_n | solution.py:386

commit v4 on v3

--- a/solution.py
+++ b/solution.py
@@ -17,7 +17,7 @@
                    obuf, hbuf, routes, ids, slots, gates, owners, goes, table, wterm,
                    p1, p2, p3, r1, r2, r3, own, ysend, yland, norm, wq, wk, wv, wo, xs, mix,
                    o_loc, o_snd, o_rcv, h_loc, h_snd, h_rcv, t_loc, t_snd, t_rcv, w_snd, w_rcv, w_loc,
-                   s1, s2, s3, q1, q2, q3, ys, yr, wt, zs):
+                   s1, s2, s3, q1, q2, q3, ys, yr, wt, zs, n_loc_sem):
     n_ep, n_st, n_loc, cap, slot_pad, seq_len, top_k, half = dims
     n_chip = n_ep // CORES
     n_half = n_ep // 2
@@ -49,6 +49,18 @@
                               obuf.at[h, pl.ds(core * n_loc, n_loc), pl.ds(0, cap)], o_loc.at[h]).start()
     h_copy = pltpu.make_async_copy(resid_ref.at[:, my_cols], hbuf.at[core], h_loc)
     h_copy.start()
+    model = CORES * half
+    strip = model // n_half
+
+    def weight(i, part):
+        src, dst = ((q_ref, wq), (k_ref, wk), (v_ref, wv), (o_ref, wo))[i]
+        rows = pl.ds(part * strip, strip)
+        return pltpu.make_async_copy(src.at[rows], dst.at[rows], wt.at[i, part])
+
+    norm_copy = pltpu.make_async_copy(norm_ref, norm, n_loc_sem)
+    norm_copy.start()
+    for part in range(n_half):
+        weight(0, part).start()
     for copy in small:
         copy.wait()
     key = jnp.where(slots[...] >= 0, ids[...] * slot_pad + slots[...] - me * cap, -1)
@@ -67,24 +79,23 @@
         t_out.append(pltpu.make_async_remote_copy(routes.at[me], routes.at[me], t_snd.at[k - 1], t_rcv.at[me],
                                                   device_id={'ep': peer}, device_id_type=MESH))
         t_out[-1].start()
-    o_out = []
-    for h in order:
-        o_out.append(pltpu.make_async_remote_copy(out_ref.at[:, pl.ds(h * cap, cap), sib_cols],
-                                                  obuf.at[h, pl.ds(core * n_loc, n_loc), pl.ds(0, cap)],
-                                                  o_snd.at[h], o_rcv.at[h],
-                                                  device_id={'ep': sib}, device_id_type=MESH))
-        o_out[-1].start()
+
+    def o_out(h):
+        return pltpu.make_async_remote_copy(out_ref.at[:, pl.ds(h * cap, cap), sib_cols],
+                                            obuf.at[h, pl.ds(core * n_loc, n_loc), pl.ds(0, cap)],
+                                            o_snd.at[h], o_rcv.at[h],
+                                            device_id={'ep': sib}, device_id_type=MESH)
+
     h_out = pltpu.make_async_remote_copy(resid_ref.at[:, sib_cols], hbuf.at[core], h_snd, h_rcv,
                                          device_id={'ep': sib}, device_id_type=MESH)
-    h_out.start()
+    for i, h in enumerate(order):
+        o_out(h).start()
+        if i == 1:
+            h_out.start()
 
     w_out.wait_recv()
     goes_copy = pltpu.make_async_copy(owners, goes, w_loc)
     goes_copy.start()
-    for k in range(1, n_ep):
-        src = lax.rem(me + k, n_ep)
-        pltpu.make_async_remote_copy(routes.at[src], routes.at[src], t_snd.at[k - 1], t_rcv.at[src],
-                                     device_id={'ep': src}, device_id_type=MESH).wait_recv()
     goes_copy.wait()
 
     def o_wait(h):
@@ -98,15 +109,17 @@
     depth = CORES * n_loc * slot_pad
     width = min(256, half)
     n_sub = half // width
-    model = CORES * half
     tile = min(512, model)
-    weights = [pltpu.make_async_copy(src, dst, wt.at[i])
-               for i, (src, dst) in enumerate(((q_ref, wq), (k_ref, wk), (v_ref, wv), (o_ref, wo), (norm_ref, norm)))]
     lane = lax.broadcasted_iota(jnp.int32, (seq_len, depth), 1).astype(jnp.float32)
     block = CORES * seq_len
 
     def partial(q, ab):
         h = q + n_half * ab
+
+        @pl.when(h != me)
+        def _():
+            pltpu.make_async_remote_copy(routes.at[h], routes.at[h], t_snd.at[0], t_rcv.at[h],
+                                         device_id={'ep': h}, device_id_type=MESH).wait_recv()
         rows = routes[h]
         rows = jnp.concatenate([rows, jnp.zeros((128 - rows.shape[0], tok_dev), jnp.float32)], axis=0)
         table[...] = rows.T
@@ -158,6 +171,11 @@
         def _():
             hc = lax.rem(h, CORES)
 
+            @pl.when(hc == 0)
+            def _():
+                h_copy.wait()
+                h_out.wait_recv()
+
             @pl.loop(0, half // width)
             def _(n):
                 cols = pl.ds(pl.multiple_of(n * width, width), width)
@@ -166,6 +184,12 @@
                     rs = slice((b % CORES) * seq_len, (b % CORES + 1) * seq_len)
                     held = chosen(pick, lambda s: hbuf[hc, s * seq_len:(s + 1) * seq_len, cols].astype(jnp.float32))
                     dst[rs, cols] = dst[rs, cols] + held
+
+    def o_out_wait(h):
+        pltpu.make_async_remote_copy(out_ref.at[:, pl.ds(0, cap), sib_cols],
+                                     obuf.at[h, pl.ds(core * n_loc, n_loc), pl.ds(0, cap)],
+                                     o_snd.at[h], o_rcv.at[h],
+                                     device_id={'ep': sib}, device_id_type=MESH).wait_send()
 
     def ring(src, dst, snd, rcv, d, q):
         return pltpu.make_async_remote_copy(src.at[d, q], dst.at[d, q], snd.at[d, q], rcv.at[d, q],
@@ -239,9 +263,6 @@
     def store(q):
         return pltpu.make_async_copy(yland.at[pl.ds(2 * q, 2)], z_ref.at[pl.ds(2 * q, 2)], zs.at[q])
 
-    h_copy.wait()
-    h_out.wait_recv()
-
     @pl.loop(0, n_half + 3)
     def _(it):
         @pl.when(it < n_half)
@@ -258,11 +279,6 @@
                         def _():
                             ring(p2, r2, s2, q2, 1 - d, it).start()
 
-        @pl.when(it == 0)
-        def _():
-            for copy in weights:
-                copy.start()
-
         @pl.when(jnp.logical_and(it >= 1, it <= n_half))
         def _():
             q = it - 1
@@ -277,10 +293,18 @@
             for d in range(2):
                 ring(p2, r2, s2, q2, d, it).start()
 
+        for i in range(1, 4):
+            @pl.when(it == i - 1)
+            def _():
+                for part in range(n_half):
+                    weight(i, part).start()
+
         @pl.when(it == 3)
         def _():
-            for copy in weights:
-                copy.wait()
+            norm_copy.wait()
+            for i in range(3):
+                for part in range(n_half):
+                    weight(i, part).wait()
 
         @pl.when(it >= 3)
         def _():
@@ -296,15 +320,26 @@
             def _():
                 finish(it - 2, n)
 
+        @pl.when(it == 3)
+        def _():
+            for part in range(n_half):
+                weight(3, part).wait()
+
+        @pl.when(it == n_half)
+        def _():
+            w_out.wait_send()
+            h_out.wait_send()
+            for copy in t_out:
+                copy.wait_send()
+
+            @pl.loop(0, n_ep)
+            def _(h):
+                o_out_wait(h)
+
         @pl.when(it >= 3)
         def _():
             project(it - 3)
             store(it - 3).start()
-
-    w_out.wait_send()
-    for copy in t_out + o_out:
-        copy.wait_send()
-    h_out.wait_send()
 
     @pl.loop(0, n_half)
     def _(q):
@@ -376,14 +411,14 @@
                 dma, dma, dma,
                 dma((2, n_half)), dma((2, n_half)), dma((2, n_half, n_sub)),
                 dma((2, n_half)), dma((2, n_half)), dma((2, n_half, n_sub)),
-                dma((n_half, CORES, n_sub)), dma((CORES, n_half, n_sub)), dma((5,)), dma((n_half,)),
+                dma((n_half, CORES, n_sub)), dma((CORES, n_half, n_sub)), dma((4, n_half)), dma((n_half,)), dma,
             ],
             compiler_params=pltpu.CompilerParams(collective_id=0, has_side_effects=True, vmem_limit_bytes=67043328),
             name='stage',
         )(owner, expert_id[0, 0].T, slot_id[0, 0].T, gate[0, 0].T, expert_out[0, 0], resid[0, 0],
           norm_w, w_q[0], w_k[0], w_v[0], w_o[0])
         source = lax.dynamic_slice_in_dim(owner[0], dev_index * seq_dev, seq_dev) // seq_dev
-        z_owned = jnp.take(z_pairs, source % n_half * 2 + source // n_half, axis=0)
+        z_owned = z_pairs.at[source % n_half * 2 + source // n_half].get(mode='promise_in_bounds', unique_indices=True)
         return z_owned.reshape(1, 1, tok_dev, model_dim)
 
     tok_spec = P(group_axes, None, 'ep', None)

time: 118 us -> 110 us (0.932)
  Pallas kernels: 111 us -> 106 us
  other arithmetic: 3.9 us -> 1.34 us
    pallas_call x1, Pallas kernels: 111 us -> 106 us  [device_step(): pl.pallas_call(functools.partial(stage_kernel, dims), out_shape=jax.Shape...]
    select_n x2 -> x1, other arithmetic: 2.55 us -> 0.74 us  [device_step(): z_pairs.at[source % n_half * 2 + source // n_half]]
where the time goes in v4:
time: 110 us
  Pallas kernels  106 us (96%)
  local copies, waits for them, and re-layouts  2.93 us (3%)
  other arithmetic  1.34 us (1%)
    pallas_call x1, Pallas kernels, device_step(): pl.pallas_call(functools.partial(stage_kernel, dims), out_shape=jax.Shape...  106 us
    gather x1, local copies, waits for them, and re-layouts, device_step(): z_pairs.at[source % n_half * 2 + source // n_half]  2.93 us

profile of v4, /device:TPU:97, one launch (start us, length us, event | category | flops | bytes accessed | tf_op | source)
XLA Modules:
  0.0 110.0 jit_solution(9380949523015414687)
XLA Ops:
  0.0 0.7 fusion.2
  0.7 0.6 pad_clamp_fusion
  1.3 105.7 %stage.1 = bf16[8,32,2048]{2,1,0:T(8,128)(2,1)} custom-call(s32[1,64]{1,0:T(1,128)} %owner_ref.1, s32[8,256]{1,0:T(8,128)} %bitcast.34, s32[8,256]{1,0:T(8,128)} %bitcast.35, f32[8,256]{1,0:T(8,128)} %bitcast.36, bf16[8,320,2048]{2,1,0:T(8,128)(2,1)} %bitcast.28, bf16[256,2048]{1,0:T(8,128)(2,1)} %bitcast.33, f32[1,2048]{1,0:T(1,128)} %norm_ref.1, ...), custom_call_target="tpu_custom_call" | custom-call | tf_op jit(solution)/shard_map/stage/pallas_call | solution.py:385
  107.1 2.9 %gather_fusion = bf16[8,32,2048]{2,1,0:T(8,128)(2,1)} fusion(bf16[8,32,2048]{2,1,0:T(8,128)(2,1)} %stage.1, s32[1024]{0:T(1024)} %pad_clamp_fusion), kind=kCustom, calls=%fused_computation | custom fusion | bytes 2097184 | tf_op jit(solution)/shard_map/gather | solution.py:421

commit v5 on v4

--- a/solution.py
+++ b/solution.py
@@ -11,6 +11,7 @@
 NORM_EPS = 1e-6
 MESH = pl.DeviceIdType.MESH
 CORES = 2
+LEGS = 1
 
 
 def stage_kernel(dims, owner_ref, id_ref, slot_ref, gate_ref, out_ref, resid_ref, norm_ref, q_ref, k_ref, v_ref, o_ref, z_ref,
@@ -108,7 +109,7 @@
 
     depth = CORES * n_loc * slot_pad
     width = min(256, half)
-    n_sub = half // width
+    leg = half // LEGS
     tile = min(512, model)
     lane = lax.broadcasted_iota(jnp.int32, (seq_len, depth), 1).astype(jnp.float32)
     block = CORES * seq_len
@@ -196,14 +197,14 @@
                                             device_id={'ep': side[d]}, device_id_type=MESH)
 
     def sub(n):
-        return pl.ds(pl.multiple_of(n * width, width), width)
+        return pl.ds(pl.multiple_of(n * leg, leg), leg)
 
     def last_leg(d, q, n):
         return pltpu.make_async_remote_copy(r1.at[d, q, :, sub(n)], r3.at[d, q, :, sub(n)], s3.at[d, q, n], q3.at[d, q, n],
                                             device_id={'ep': side[d]}, device_id_type=MESH)
 
     def hop(q, jc, n, c, to):
-        cols = pl.ds(pl.multiple_of(c * half + n * width, width), width)
+        cols = pl.ds(pl.multiple_of(c * half + n * leg, leg), leg)
         return pltpu.make_async_remote_copy(ysend.at[q, jc, :, :, sub(n)], yland.at[pl.ds(2 * q, 2), :, cols],
                                             ys.at[q, jc, n], yr.at[c, q, n],
                                             device_id={'pp': nxt, 'ep': to}, device_id_type=MESH)
@@ -231,7 +232,7 @@
 
     def normalise(q):
         for c in range(CORES):
-            for n in range(n_sub):
+            for n in range(LEGS):
                 hop(q, 0, n, c, me).wait_recv()
         for ab in range(2):
             y = yland[2 * q + ab].astype(jnp.float32)
@@ -285,7 +286,7 @@
             for d in range(2):
                 ring(p1, r1, s1, q1, d, q).wait_recv()
                 r1[d, q] = p3[d, lax.rem(q, 2)] + r1[d, q]
-                for n in range(n_sub):
+                for n in range(LEGS):
                     last_leg(d, q, n).start()
 
         @pl.when(jnp.logical_and(it >= 1, it < n_half))
@@ -310,14 +311,16 @@
         def _():
             normalise(it - 3)
 
-        @pl.loop(0, n_sub)
-        def _(n):
-            @pl.when(it >= 3)
-            def _():
+        @pl.when(it >= 3)
+        def _():
+            @pl.loop(0, model // tile)
+            def _(n):
                 attend(n)
 
-            @pl.when(jnp.logical_and(it >= 2, it < n_half + 2))
-            def _():
+        @pl.when(jnp.logical_and(it >= 2, it < n_half + 2))
+        def _():
+            @pl.loop(0, LEGS)
+            def _(n):
                 finish(it - 2, n)
 
         @pl.when(it == 3)
@@ -346,10 +349,10 @@
         for d in range(2):
             ring(p1, r1, s1, q1, d, q).wait_send()
             ring(p2, r2, s2, q2, d, q).wait_send()
-            for n in range(n_sub):
+            for n in range(LEGS):
                 last_leg(d, q, n).wait_send()
         for jc in range(CORES):
-            for n in range(n_sub):
+            for n in range(LEGS):
                 hop(q, jc, n, core, chip * CORES + jc).wait_send()
         store(q).wait()
 
@@ -374,8 +377,7 @@
 
         dims = (n_ep, n_stages, n_loc, cap, slot_pad, seq_len, top_k, half)
         f32, bf16 = jnp.float32, jnp.bfloat16
-        n_sub = half // min(256, half)
-        assert model_dim // min(512, model_dim) == n_sub and n_half > 3
+        assert n_half > 3
 
         def ringbuf(slots):
             return pltpu.VMEM((2, slots, block, half), f32)
@@ -409,9 +411,9 @@
                 dma, dma, dma,
                 dma((3,)), dma((n_ep - 1,)), dma((n_ep,)),
                 dma, dma, dma,
-                dma((2, n_half)), dma((2, n_half)), dma((2, n_half, n_sub)),
-                dma((2, n_half)), dma((2, n_half)), dma((2, n_half, n_sub)),
-                dma((n_half, CORES, n_sub)), dma((CORES, n_half, n_sub)), dma((4, n_half)), dma((n_half,)), dma,
+                dma((2, n_half)), dma((2, n_half)), dma((2, n_half, LEGS)),
+                dma((2, n_half)), dma((2, n_half)), dma((2, n_half, LEGS)),
+                dma((n_half, CORES, LEGS)), dma((CORES, n_half, LEGS)), dma((4, n_half)), dma((n_half,)), dma,
             ],
             compiler_params=pltpu.CompilerParams(collective_id=0, has_side_effects=True, vmem_limit_bytes=67043328),
             name='stage',

time: 110 us -> 115 us (1.045)
  Pallas kernels: 106 us -> 111 us
    pallas_call x1, Pallas kernels: 106 us -> 111 us  [device_step(): pl.pallas_call(functools.partial(stage_kernel, dims), out_shape=jax.Shape...]
where the time goes in v5:
time: 115 us
  Pallas kernels  111 us (97%)
  local copies, waits for them, and re-layouts  2.93 us (3%)
  other arithmetic  1.34 us (1%)
    pallas_call x1, Pallas kernels, device_step(): pl.pallas_call(functools.partial(stage_kernel, dims), out_shape=jax.Shape...  111 us
    gather x1, local copies, waits for them, and re-layouts, device_step(): z_pairs.at[source % n_half * 2 + source // n_half]  2.93 us

profile of v5, /device:TPU:97, one launch (start us, length us, event | category | flops | bytes accessed | tf_op | source)
XLA Modules:
  0.0 115.4 jit_solution(7291899329462371006)
XLA Ops:
  0.0 0.7 fusion.2
  0.7 0.6 pad_clamp_fusion
  1.3 111.1 %stage.1 = bf16[8,32,2048]{2,1,0:T(8,128)(2,1)} custom-call(s32[1,64]{1,0:T(1,128)} %owner_ref.1, s32[8,256]{1,0:T(8,128)} %bitcast.34, s32[8,256]{1,0:T(8,128)} %bitcast.35, f32[8,256]{1,0:T(8,128)} %bitcast.36, bf16[8,320,2048]{2,1,0:T(8,128)(2,1)} %bitcast.28, bf16[256,2048]{1,0:T(8,128)(2,1)} %bitcast.33, f32[1,2048]{1,0:T(1,128)} %norm_ref.1, ...), custom_call_target="tpu_custom_call" | custom-call | tf_op jit(solution)/shard_map/stage/pallas_call | solution.py:387
  112.4 2.9 %gather_fusion = bf16[8,32,2048]{2,1,0:T(8,128)(2,1)} fusion(bf16[8,32,2048]{2,1,0:T(8,128)(2,1)} %stage.1, s32[1024]{0:T(1024)} %pad_clamp_fusion), kind=kCustom, calls=%fused_computation | custom fusion | bytes 2097184 | tf_op jit(solution)/shard_map/gather | solution.py:423

commit v6 on v4

--- a/solution.py
+++ b/solution.py
@@ -14,10 +14,10 @@
 
 
 def stage_kernel(dims, owner_ref, id_ref, slot_ref, gate_ref, out_ref, resid_ref, norm_ref, q_ref, k_ref, v_ref, o_ref, z_ref,
-                   obuf, hbuf, routes, ids, slots, gates, owners, goes, table, wterm,
+                   obuf, hbuf, routes, ids, slots, gates, owners, goes, comes, table, wterm,
                    p1, p2, p3, r1, r2, r3, own, ysend, yland, norm, wq, wk, wv, wo, xs, mix,
                    o_loc, o_snd, o_rcv, h_loc, h_snd, h_rcv, t_loc, t_snd, t_rcv, w_snd, w_rcv, w_loc,
-                   s1, s2, s3, q1, q2, q3, ys, yr, wt, zs, n_loc_sem):
+                   s1, s2, s3, q1, q2, q3, ys, yr, wt, zs, n_loc_sem, c_loc):
     n_ep, n_st, n_loc, cap, slot_pad, seq_len, top_k, half = dims
     n_chip = n_ep // CORES
     n_half = n_ep // 2
@@ -59,8 +59,8 @@
 
     norm_copy = pltpu.make_async_copy(norm_ref, norm, n_loc_sem)
     norm_copy.start()
-    for part in range(n_half):
-        weight(0, part).start()
+    comes_copy = pltpu.make_async_copy(owner_ref, comes, c_loc)
+    comes_copy.start()
     for copy in small:
         copy.wait()
     key = jnp.where(slots[...] >= 0, ids[...] * slot_pad + slots[...] - me * cap, -1)
@@ -81,17 +81,16 @@
         t_out[-1].start()
 
     def o_out(h):
-        return pltpu.make_async_remote_copy(out_ref.at[:, pl.ds(h * cap, cap), sib_cols],
+        return pltpu.make_async_remote_copy(out_ref.at[:, pl.ds(pl.multiple_of(h * cap, 8), cap), sib_cols],
                                             obuf.at[h, pl.ds(core * n_loc, n_loc), pl.ds(0, cap)],
                                             o_snd.at[h], o_rcv.at[h],
                                             device_id={'ep': sib}, device_id_type=MESH)
 
     h_out = pltpu.make_async_remote_copy(resid_ref.at[:, sib_cols], hbuf.at[core], h_snd, h_rcv,
                                          device_id={'ep': sib}, device_id_type=MESH)
-    for i, h in enumerate(order):
-        o_out(h).start()
-        if i == 1:
-            h_out.start()
+    for ab in range(2):
+        o_out(n_half * ab).start()
+    h_out.start()
 
     w_out.wait_recv()
     goes_copy = pltpu.make_async_copy(owners, goes, w_loc)
@@ -106,12 +105,18 @@
                                      o_snd.at[h], o_rcv.at[h],
                                      device_id={'ep': sib}, device_id_type=MESH).wait_recv()
 
+    def ring(src, dst, snd, rcv, d, q):
+        return pltpu.make_async_remote_copy(src.at[d, q], dst.at[d, q], snd.at[d, q], rcv.at[d, q],
+                                            device_id={'ep': side[d]}, device_id_type=MESH)
+
     depth = CORES * n_loc * slot_pad
     width = min(256, half)
-    n_sub = half // width
-    tile = min(512, model)
+    tile = min(512, half)
+    n_sub = model // tile
+    leg = half // n_sub
     lane = lax.broadcasted_iota(jnp.int32, (seq_len, depth), 1).astype(jnp.float32)
     block = CORES * seq_len
+    per = n_chip * CORES // 2
 
     def partial(q, ab):
         h = q + n_half * ab
@@ -142,48 +147,61 @@
             return got
 
         base = (chip * depth).astype(jnp.float32)
-        for b, pick in enumerate(picks):
-            rt = chosen(pick, lambda s: table[s * seq_len:(s + 1) * seq_len, :])
-            w = jnp.zeros((seq_len, depth), jnp.float32)
-            for j in range(top_k):
-                key = rt[:, j:j + 1] - base
-                w = jnp.where(lane == key, rt[:, top_k + j:top_k + j + 1], w)
-            hi = w.astype(jnp.bfloat16)
-            rest = w - hi.astype(jnp.float32)
-            mid = rest.astype(jnp.bfloat16)
-            low = (rest - mid.astype(jnp.float32)).astype(jnp.bfloat16)
-            for t, term in enumerate((hi, mid, low)):
-                wterm[pl.ds(t * tok_dev + b * seq_len, seq_len), :] = term
-
         dsts = [p1.at[ab, q], p2.at[1 - ab, q], p3.at[ab, lax.rem(q, 2)], own.at[ab, lax.rem(q, 3)]]
-        o_wait(h)
-
-        @pl.loop(0, half // width)
-        def _(n):
-            cols = pl.ds(pl.multiple_of(n * width, width), width)
-            slots_in = obuf[h, :, :, cols].reshape(depth, width)
-            res = jnp.dot(wterm[...], slots_in, preferred_element_type=jnp.float32)
-            res = res[:tok_dev] + (res[tok_dev:2 * tok_dev] + res[2 * tok_dev:])
-            for r in range(n_chip):
-                dsts[r][:, cols] = res[r * block:(r + 1) * block]
-
-        @pl.when(h // CORES == chip)
-        def _():
-            hc = lax.rem(h, CORES)
-
-            @pl.when(hc == 0)
-            def _():
-                h_copy.wait()
-                h_out.wait_recv()
+        for part in range(2):
+            mine = picks[part * per:(part + 1) * per]
+            for b, pick in enumerate(mine):
+                rt = chosen(pick, lambda s: table[s * seq_len:(s + 1) * seq_len, :])
+                w = jnp.zeros((seq_len, depth), jnp.float32)
+                for j in range(top_k):
+                    key = rt[:, j:j + 1] - base
+                    w = jnp.where(lane == key, rt[:, top_k + j:top_k + j + 1], w)
+                hi = w.astype(jnp.bfloat16)
+                rest = w - hi.astype(jnp.float32)
+                mid = rest.astype(jnp.bfloat16)
+                low = (rest - mid.astype(jnp.float32)).astype(jnp.bfloat16)
+                for t, term in enumerate((hi, mid, low)):
+                    wterm[pl.ds((t * per + b) * seq_len, seq_len), :] = term
+            if part == 0:
+                o_wait(h)
 
             @pl.loop(0, half // width)
             def _(n):
                 cols = pl.ds(pl.multiple_of(n * width, width), width)
-                for b, pick in enumerate(picks):
-                    dst = dsts[b // CORES]
-                    rs = slice((b % CORES) * seq_len, (b % CORES + 1) * seq_len)
-                    held = chosen(pick, lambda s: hbuf[hc, s * seq_len:(s + 1) * seq_len, cols].astype(jnp.float32))
-                    dst[rs, cols] = dst[rs, cols] + held
+                slots_in = obuf[h, :, :, cols].reshape(depth, width)
+                res = jnp.dot(wterm[...], slots_in, preferred_element_type=jnp.float32)
+                span = per * seq_len
+                res = res[:span] + (res[span:2 * span] + res[2 * span:])
+                for r in range(2):
+                    dsts[2 * part + r][:, cols] = res[r * block:(r + 1) * block]
+
+            @pl.when(h // CORES == chip)
+            def _():
+                hc = lax.rem(h, CORES)
+                if part == 0:
+                    @pl.when(hc == 0)
+                    def _():
+                        h_copy.wait()
+                        h_out.wait_recv()
+
+                @pl.loop(0, half // width)
+                def _(n):
+                    cols = pl.ds(pl.multiple_of(n * width, width), width)
+                    for b, pick in enumerate(mine):
+                        dst = dsts[2 * part + b // CORES]
+                        rs = slice((b % CORES) * seq_len, (b % CORES + 1) * seq_len)
+                        held = chosen(pick, lambda s: hbuf[hc, s * seq_len:(s + 1) * seq_len, cols].astype(jnp.float32))
+                        dst[rs, cols] = dst[rs, cols] + held
+
+            if part == 0:
+                for d in range(2):
+                    @pl.when(jnp.logical_and(ab == d, q <= 1))
+                    def _():
+                        ring(p1, r1, s1, q1, d, q).start()
+
+                    @pl.when(jnp.logical_and(ab == d, q == 0))
+                    def _():
+                        ring(p2, r2, s2, q2, 1 - d, q).start()
 
     def o_out_wait(h):
         pltpu.make_async_remote_copy(out_ref.at[:, pl.ds(0, cap), sib_cols],
@@ -191,19 +209,15 @@
                                      o_snd.at[h], o_rcv.at[h],
                                      device_id={'ep': sib}, device_id_type=MESH).wait_send()
 
-    def ring(src, dst, snd, rcv, d, q):
-        return pltpu.make_async_remote_copy(src.at[d, q], dst.at[d, q], snd.at[d, q], rcv.at[d, q],
-                                            device_id={'ep': side[d]}, device_id_type=MESH)
-
     def sub(n):
-        return pl.ds(pl.multiple_of(n * width, width), width)
+        return pl.ds(pl.multiple_of(n * leg, leg), leg)
 
     def last_leg(d, q, n):
         return pltpu.make_async_remote_copy(r1.at[d, q, :, sub(n)], r3.at[d, q, :, sub(n)], s3.at[d, q, n], q3.at[d, q, n],
                                             device_id={'ep': side[d]}, device_id_type=MESH)
 
     def hop(q, jc, n, c, to):
-        cols = pl.ds(pl.multiple_of(c * half + n * width, width), width)
+        cols = pl.ds(pl.multiple_of(c * half + n * leg, leg), leg)
         return pltpu.make_async_remote_copy(ysend.at[q, jc, :, :, sub(n)], yland.at[pl.ds(2 * q, 2), :, cols],
                                             ys.at[q, jc, n], yr.at[c, q, n],
                                             device_id={'pp': nxt, 'ep': to}, device_id_type=MESH)
@@ -252,16 +266,37 @@
             mix[:, pl.ds(pl.multiple_of(n * tile + hd * HEAD_DIM, HEAD_DIM), HEAD_DIM)] = mixed
 
     def project(q):
-        @pl.loop(0, model // tile)
-        def _(n):
-            cols = pl.ds(pl.multiple_of(n * tile, tile), tile)
-            out = jnp.dot(mix[...], wo[:, cols], preferred_element_type=jnp.float32).astype(jnp.bfloat16).astype(jnp.float32)
-            for ab in range(2):
-                y = yland[2 * q + ab, :, cols].astype(jnp.float32)
-                yland[2 * q + ab, :, cols] = (y + out[ab * seq_len:(ab + 1) * seq_len]).astype(jnp.bfloat16)
-
-    def store(q):
-        return pltpu.make_async_copy(yland.at[pl.ds(2 * q, 2)], z_ref.at[pl.ds(2 * q, 2)], zs.at[q])
+        @pl.loop(0, CORES)
+        def _(c):
+            @pl.loop(0, half // tile)
+            def _(n):
+                cols = pl.ds(pl.multiple_of(c * half + n * tile, tile), tile)
+                out = jnp.dot(mix[...], wo[:, cols], preferred_element_type=jnp.float32).astype(jnp.bfloat16).astype(jnp.float32)
+                z = []
+                for ab in range(2):
+                    y = yland[2 * q + ab, :, cols].astype(jnp.float32)
+                    z.append((y + out[ab * seq_len:(ab + 1) * seq_len]).astype(jnp.bfloat16))
+                cols = pl.ds(pl.multiple_of(n * tile, tile), tile)
+                for b in range(n_ep):
+                    home = comes[0, me * n_ep + b] // n_ep
+                    rs = pl.ds(b * seq_len, seq_len)
+                    hbuf[c, rs, cols] = jnp.where(home == q, z[0], jnp.where(home == q + n_half, z[1], hbuf[c, rs, cols]))
+
+    def store(c):
+        return pltpu.make_async_copy(hbuf.at[c], z_ref.at[:, pl.ds(c * half, half)], zs.at[c])
+
+    def last(q):
+        for d in range(2):
+            ring(p1, r1, s1, q1, d, q).wait_recv()
+            r1[d, q] = p3[d, lax.rem(q, 2)] + r1[d, q]
+            for n in range(n_sub):
+                last_leg(d, q, n).start()
+
+    def first(q):
+        for d in range(2):
+            ring(p1, r1, s1, q1, d, q).start()
+        for d in range(2):
+            ring(p2, r2, s2, q2, d, q).start()
 
     @pl.loop(0, n_half + 3)
     def _(it):
@@ -270,31 +305,25 @@
             @pl.loop(0, 2)
             def _(ab):
                 partial(it, ab)
-                for d in range(2):
-                    @pl.when(ab == d)
-                    def _():
-                        ring(p1, r1, s1, q1, d, it).start()
-
-                        @pl.when(it == 0)
-                        def _():
-                            ring(p2, r2, s2, q2, 1 - d, it).start()
-
-        @pl.when(jnp.logical_and(it >= 1, it <= n_half))
-        def _():
-            q = it - 1
+
+                @pl.when(jnp.logical_and(ab == 0, it < n_half - 1))
+                def _():
+                    for other in range(2):
+                        o_out(it + 1 + n_half * other).start()
+
+        @pl.when(it == 1)
+        def _():
+            last(0)
             for d in range(2):
-                ring(p1, r1, s1, q1, d, q).wait_recv()
-                r1[d, q] = p3[d, lax.rem(q, 2)] + r1[d, q]
-                for n in range(n_sub):
-                    last_leg(d, q, n).start()
-
-        @pl.when(jnp.logical_and(it >= 1, it < n_half))
-        def _():
-            for d in range(2):
-                ring(p2, r2, s2, q2, d, it).start()
-
-        for i in range(1, 4):
-            @pl.when(it == i - 1)
+                ring(p2, r2, s2, q2, d, 1).start()
+            last(1)
+
+        @pl.when(it == 2)
+        def _():
+            first(2)
+
+        for i in range(4):
+            @pl.when(it == (0, 1, 1, 2)[i])
             def _():
                 for part in range(n_half):
                     weight(i, part).start()
@@ -302,6 +331,7 @@
         @pl.when(it == 3)
         def _():
             norm_copy.wait()
+            comes_copy.wait()
             for i in range(3):
                 for part in range(n_half):
                     weight(i, part).wait()
@@ -324,6 +354,8 @@
         def _():
             for part in range(n_half):
                 weight(3, part).wait()
+            last(2)
+            first(3)
 
         @pl.when(it == n_half)
         def _():
@@ -339,7 +371,13 @@
         @pl.when(it >= 3)
         def _():
             project(it - 3)
-            store(it - 3).start()
+
+        @pl.when(it == 4)
+        def _():
+            last(3)
+
+    for c in range(CORES):
+        store(c).start()
 
     @pl.loop(0, n_half)
     def _(q):
@@ -351,7 +389,8 @@
         for jc in range(CORES):
             for n in range(n_sub):
                 hop(q, jc, n, core, chip * CORES + jc).wait_send()
-        store(q).wait()
+    for c in range(CORES):
+        store(c).wait()
 
 
 def solution(mesh):
@@ -360,7 +399,6 @@
     group_axes = ('data', 'pp')
 
     def device_step(expert_out, expert_id, slot_id, gate, resid, owner, norm_w, w_q, w_k, w_v, w_o):
-        dev_index = lax.axis_index('ep')
         n_loc, capacity, model_dim = expert_out.shape[2:]
         cap = capacity // n_ep
         tok_dev, top_k = expert_id.shape[2:]
@@ -374,17 +412,17 @@
 
         dims = (n_ep, n_stages, n_loc, cap, slot_pad, seq_len, top_k, half)
         f32, bf16 = jnp.float32, jnp.bfloat16
-        n_sub = half // min(256, half)
-        assert model_dim // min(512, model_dim) == n_sub and n_half > 3
+        n_sub = model_dim // min(512, half)
+        assert n_half == 4
 
         def ringbuf(slots):
             return pltpu.VMEM((2, slots, block, half), f32)
 
         square = pltpu.VMEM((model_dim, model_dim), bf16)
         dma = pltpu.SemaphoreType.DMA
-        z_pairs = pl.pallas_call(
+        z_owned = pl.pallas_call(
             functools.partial(stage_kernel, dims),
-            out_shape=jax.ShapeDtypeStruct((n_ep, seq_len, model_dim), bf16),
+            out_shape=jax.ShapeDtypeStruct((tok_dev, model_dim), bf16),
             in_specs=[pl.BlockSpec(memory_space=pl.ANY)] * 11,
             out_specs=pl.BlockSpec(memory_space=pl.ANY),
             scratch_shapes=[
@@ -396,8 +434,9 @@
                 pltpu.VMEM((top_k, tok_dev), f32),
                 pltpu.VMEM((1, n_ep * seq_dev), jnp.int32),
                 pltpu.SMEM((1, n_ep * seq_dev), jnp.int32),
+                pltpu.SMEM((1, n_ep * seq_dev), jnp.int32),
                 pltpu.VMEM((tok_dev, 128), f32),
-                pltpu.VMEM((3 * tok_dev, CORES * n_loc * slot_pad), bf16),
+                pltpu.VMEM((3 * tok_dev // 2, CORES * n_loc * slot_pad), bf16),
                 ringbuf(n_half), ringbuf(n_half), ringbuf(2), ringbuf(n_half), ringbuf(n_half), ringbuf(n_half), ringbuf(3),
                 pltpu.VMEM((n_half, CORES, 2, seq_len, half), bf16),
                 pltpu.VMEM((n_ep, seq_len, model_dim), bf16),
@@ -411,14 +450,12 @@
                 dma, dma, dma,
                 dma((2, n_half)), dma((2, n_half)), dma((2, n_half, n_sub)),
                 dma((2, n_half)), dma((2, n_half)), dma((2, n_half, n_sub)),
-                dma((n_half, CORES, n_sub)), dma((CORES, n_half, n_sub)), dma((4, n_half)), dma((n_half,)), dma,
+                dma((n_half, CORES, n_sub)), dma((CORES, n_half, n_sub)), dma((4, n_half)), dma((CORES,)), dma, dma,
             ],
             compiler_params=pltpu.CompilerParams(collective_id=0, has_side_effects=True, vmem_limit_bytes=67043328),
             name='stage',
         )(owner, expert_id[0, 0].T, slot_id[0, 0].T, gate[0, 0].T, expert_out[0, 0], resid[0, 0],
           norm_w, w_q[0], w_k[0], w_v[0], w_o[0])
-        source = lax.dynamic_slice_in_dim(owner[0], dev_index * seq_dev, seq_dev) // seq_dev
-        z_owned = z_pairs.at[source % n_half * 2 + source // n_half].get(mode='promise_in_bounds', unique_indices=True)
         return z_owned.reshape(1, 1, tok_dev, model_dim)
 
     tok_spec = P(group_axes, None, 'ep', None)

time: 110 us -> 108 us (0.982)
  other arithmetic: 1.34 us -> 0 us
    gather x1 -> x0, local copies, waits for them, and re-layouts: 2.93 us -> none  [device_step(): z_pairs.at[source % n_half * 2 + source // n_half]]
    unnamed x0 -> x1, local copies, waits for them, and re-layouts: none -> 2.3 us
where the time goes in v6:
time: 108 us
  Pallas kernels  105 us (97%)
  local copies, waits for them, and re-layouts  2.3 us (2%)
    pallas_call x1, Pallas kernels, device_step(): pl.pallas_call(functools.partial(stage_kernel, dims), out_shape=jax.Shape...  105 us
    unnamed x1, local copies, waits for them, and re-layouts  2.3 us

profile of v6, /device:TPU:97, one launch (start us, length us, event | category | flops | bytes accessed | tf_op | source)
XLA Modules:
  0.0 107.6 jit_solution(16846534052510213345)
XLA Ops:
  0.0 105.3 %stage.1 = bf16[256,2048]{1,0:T(8,128)(2,1)} custom-call(s32[1,64]{1,0:T(1,128)} %owner_ref.1, s32[8,256]{1,0:T(8,128)} %bitcast.23, s32[8,256]{1,0:T(8,128)} %bitcast.24, f32[8,256]{1,0:T(8,128)} %bitcast.25, bf16[8,320,2048]{2,1,0:T(8,128)(2,1)} %bitcast.16, bf16[256,2048]{1,0:T(8,128)(2,1)} %bitcast.22, f32[1,2048]{1,0:T(1,128)} %norm_ref.1, ...), custom_call_target="tpu_custom_call" | custom-call | tf_op jit(solution)/shard_map/stage/pallas_call | solution.py:423
  105.3 2.3 %copy.13 = bf16[1,1,256,2048]{3,2,1,0:T(8,128)(2,1)} copy(bf16[1,1,256,2048]{3,2,1,0:T(8,128)(2,1)} %bitcast.21) | data formatting | bytes 2097152

commit v7 on v6

--- a/solution.py
+++ b/solution.py
@@ -14,7 +14,7 @@
 
 
 def stage_kernel(dims, owner_ref, id_ref, slot_ref, gate_ref, out_ref, resid_ref, norm_ref, q_ref, k_ref, v_ref, o_ref, z_ref,
-                   obuf, hbuf, routes, ids, slots, gates, owners, goes, comes, table, wterm,
+                   obuf, hbuf, ids, slots, gates, owners, goes, comes, table, wterm,
                    p1, p2, p3, r1, r2, r3, own, ysend, yland, norm, wq, wk, wv, wo, xs, mix,
                    o_loc, o_snd, o_rcv, h_loc, h_snd, h_rcv, t_loc, t_snd, t_rcv, w_snd, w_rcv, w_loc,
                    s1, s2, s3, q1, q2, q3, ys, yr, wt, zs, n_loc_sem, c_loc):
@@ -34,19 +34,21 @@
     sib_cols = pl.ds(pl.multiple_of((1 - core) * half, 128), half)
     order = [q + n_half * ab for q in range(n_half) for ab in range(2)]
 
-    small = [pltpu.make_async_copy(src, dst, t_loc.at[i])
-             for i, (src, dst) in enumerate(((id_ref, ids), (slot_ref, slots), (gate_ref, gates)))]
-    for copy in small:
-        copy.start()
+    raw = ((id_ref, ids), (slot_ref, slots), (gate_ref, gates))
+    for i, (src, dst) in enumerate(raw):
+        pltpu.make_async_copy(src, dst.at[me], t_loc.at[i]).start()
     barrier = pltpu.get_barrier_semaphore()
     for k in range(1, n_ep):
         pl.semaphore_signal(barrier, inc=1, device_id={'ep': lax.rem(me + k, n_ep)}, device_id_type=MESH)
     for other in (nxt, prv):
         for jc in range(CORES):
             pl.semaphore_signal(barrier, inc=1, device_id={'pp': other, 'ep': chip * CORES + jc}, device_id_type=MESH)
-    for h in order:
-        pltpu.make_async_copy(out_ref.at[:, pl.ds(h * cap, cap), my_cols],
-                              obuf.at[h, pl.ds(core * n_loc, n_loc), pl.ds(0, cap)], o_loc.at[h]).start()
+    def o_in(h):
+        return pltpu.make_async_copy(out_ref.at[:, pl.ds(h * cap, cap), my_cols],
+                                     obuf.at[h, pl.ds(core * n_loc, n_loc), pl.ds(0, cap)], o_loc.at[h])
+
+    for h in order[:2]:
+        o_in(h).start()
     h_copy = pltpu.make_async_copy(resid_ref.at[:, my_cols], hbuf.at[core], h_loc)
     h_copy.start()
     model = CORES * half
@@ -61,11 +63,11 @@
     norm_copy.start()
     comes_copy = pltpu.make_async_copy(owner_ref, comes, c_loc)
     comes_copy.start()
-    for copy in small:
-        copy.wait()
-    key = jnp.where(slots[...] >= 0, ids[...] * slot_pad + slots[...] - me * cap, -1)
-    routes[me, :top_k] = key.astype(jnp.float32)
-    routes[me, top_k:] = gates[...]
+    for i in range(4):
+        for part in range(n_half):
+            weight(i, part).start()
+    for h in order[2:]:
+        o_in(h).start()
     if slot_pad > cap:
         for h in range(n_ep):
             obuf[h, :, cap:, :] = jnp.zeros((CORES * n_loc, slot_pad - cap, half), jnp.bfloat16)
@@ -73,12 +75,15 @@
 
     w_out = pltpu.make_async_remote_copy(owner_ref, owners, w_snd, w_rcv, device_id={'pp': prv}, device_id_type=MESH)
     w_out.start()
-    t_out = []
-    for k in (n_chip, n_chip - 1, n_chip + 1, 2, n_ep - 2, 1, n_ep - 1):
-        peer = lax.rem(me + k, n_ep)
-        t_out.append(pltpu.make_async_remote_copy(routes.at[me], routes.at[me], t_snd.at[k - 1], t_rcv.at[me],
-                                                  device_id={'ep': peer}, device_id_type=MESH))
-        t_out[-1].start()
+    def route(i, k, home, peer):
+        src, dst = raw[i]
+        return pltpu.make_async_remote_copy(src, dst.at[home], t_snd.at[i, k - 1], t_rcv.at[i, home],
+                                            device_id={'ep': peer}, device_id_type=MESH)
+
+    t_out = [route(i, k, me, lax.rem(me + k, n_ep))
+             for k in (n_chip, n_chip - 1, n_chip + 1, 2, n_ep - 2, 1, n_ep - 1) for i in range(3)]
+    for copy in t_out:
+        copy.start()
 
     def o_out(h):
         return pltpu.make_async_remote_copy(out_ref.at[:, pl.ds(pl.multiple_of(h * cap, 8), cap), sib_cols],
@@ -123,10 +128,16 @@
 
         @pl.when(h != me)
         def _():
-            pltpu.make_async_remote_copy(routes.at[h], routes.at[h], t_snd.at[0], t_rcv.at[h],
-                                         device_id={'ep': h}, device_id_type=MESH).wait_recv()
-        rows = routes[h]
-        rows = jnp.concatenate([rows, jnp.zeros((128 - rows.shape[0], tok_dev), jnp.float32)], axis=0)
+            for i in range(3):
+                route(i, 1, h, h).wait_recv()
+
+        @pl.when(h == me)
+        def _():
+            for i, (src, dst) in enumerate(raw):
+                pltpu.make_async_copy(src, dst.at[me], t_loc.at[i]).wait()
+
+        key = jnp.where(slots[h] >= 0, ids[h] * slot_pad + slots[h] - h * cap, -1).astype(jnp.float32)
+        rows = jnp.concatenate([key, gates[h], jnp.zeros((128 - 2 * top_k, tok_dev), jnp.float32)], axis=0)
         table[...] = rows.T
         step = 1 - 2 * ab
         dest = [chip + 2, chip + n_chip + step, chip + n_chip - step, chip]
@@ -322,12 +333,6 @@
         def _():
             first(2)
 
-        for i in range(4):
-            @pl.when(it == (0, 1, 1, 2)[i])
-            def _():
-                for part in range(n_half):
-                    weight(i, part).start()
-
         @pl.when(it == 3)
         def _():
             norm_copy.wait()
@@ -428,10 +433,9 @@
             scratch_shapes=[
                 pltpu.VMEM((n_ep, CORES * n_loc, slot_pad, half), bf16),
                 pltpu.VMEM((CORES, tok_dev, half), bf16),
-                pltpu.VMEM((n_ep, 2 * top_k, tok_dev), f32),
-                pltpu.VMEM((top_k, tok_dev), jnp.int32),
-                pltpu.VMEM((top_k, tok_dev), jnp.int32),
-                pltpu.VMEM((top_k, tok_dev), f32),
+                pltpu.VMEM((n_ep, top_k, tok_dev), jnp.int32),
+                pltpu.VMEM((n_ep, top_k, tok_dev), jnp.int32),
+                pltpu.VMEM((n_ep, top_k, tok_dev), f32),
                 pltpu.VMEM((1, n_ep * seq_dev), jnp.int32),
                 pltpu.SMEM((1, n_ep * seq_dev), jnp.int32),
                 pltpu.SMEM((1, n_ep * seq_dev), jnp.int32),
@@ -446,7 +450,7 @@
                 pltpu.VMEM((2 * seq_len, model_dim), bf16),
                 dma((n_ep,)), dma((n_ep,)), dma((n_ep,)),
                 dma, dma, dma,
-                dma((3,)), dma((n_ep - 1,)), dma((n_ep,)),
+                dma((3,)), dma((3, n_ep - 1)), dma((3, n_ep)),
                 dma, dma, dma,
                 dma((2, n_half)), dma((2, n_half)), dma((2, n_half, n_sub)),
                 dma((2, n_half)), dma((2, n_half)), dma((2, n_half, n_sub)),

time: 108 us -> 109 us (level)
  Pallas kernels: 105 us -> 107 us
    pallas_call x1, Pallas kernels: 105 us -> 107 us  [device_step(): pl.pallas_call(functools.partial(stage_kernel, dims), out_shape=jax.Shape...]
where the time goes in v7:
time: 109 us
  Pallas kernels  107 us (98%)
  local copies, waits for them, and re-layouts  2.3 us (2%)
    pallas_call x1, Pallas kernels, device_step(): pl.pallas_call(functools.partial(stage_kernel, dims), out_shape=jax.Shape...  107 us
    unnamed x1, local copies, waits for them, and re-layouts  2.3 us

profile of v7, /device:TPU:97, one launch (start us, length us, event | category | flops | bytes accessed | tf_op | source)
XLA Modules:
  0.0 109.2 jit_solution(17776928297898305842)
XLA Ops:
  0.0 106.9 %stage.1 = bf16[256,2048]{1,0:T(8,128)(2,1)} custom-call(s32[1,64]{1,0:T(1,128)} %owner_ref.1, s32[8,256]{1,0:T(8,128)} %bitcast.23, s32[8,256]{1,0:T(8,128)} %bitcast.24, f32[8,256]{1,0:T(8,128)} %bitcast.25, bf16[8,320,2048]{2,1,0:T(8,128)(2,1)} %bitcast.16, bf16[256,2048]{1,0:T(8,128)(2,1)} %bitcast.22, f32[1,2048]{1,0:T(1,128)} %norm_ref.1, ...), custom_call_target="tpu_custom_call" | custom-call | tf_op jit(solution)/shard_map/stage/pallas_call | solution.py:428
  106.9 2.3 %copy.13 = bf16[1,1,256,2048]{3,2,1,0:T(8,128)(2,1)} copy(bf16[1,1,256,2048]{3,2,1,0:T(8,128)(2,1)} %bitcast.21) | data formatting | bytes 2097152

commit v8 on v7

--- a/solution.py
+++ b/solution.py
@@ -63,11 +63,11 @@
     norm_copy.start()
     comes_copy = pltpu.make_async_copy(owner_ref, comes, c_loc)
     comes_copy.start()
-    for i in range(4):
+    for h in order[2:]:
+        o_in(h).start()
+    for i in range(2):
         for part in range(n_half):
             weight(i, part).start()
-    for h in order[2:]:
-        o_in(h).start()
     if slot_pad > cap:
         for h in range(n_ep):
             obuf[h, :, cap:, :] = jnp.zeros((CORES * n_loc, slot_pad - cap, half), jnp.bfloat16)
@@ -250,8 +250,9 @@
             hop(q, jc, n, core, chip * CORES + jc).start()
 
     n_tok = 2 * seq_len
-    row = lax.broadcasted_iota(jnp.int32, (n_tok, n_tok), 0)
-    col = lax.broadcasted_iota(jnp.int32, (n_tok, n_tok), 1)
+    n_row = tile // HEAD_DIM * n_tok
+    row = lax.broadcasted_iota(jnp.int32, (n_row, n_tok), 0) % n_tok
+    col = lax.broadcasted_iota(jnp.int32, (n_row, n_tok), 1)
     causal = jnp.logical_and(row >= col, row // seq_len == col // seq_len)
 
     def normalise(q):
@@ -263,18 +264,26 @@
             inv = lax.rsqrt(jnp.mean(y * y, axis=-1, keepdims=True) + NORM_EPS)
             xs[ab * seq_len:(ab + 1) * seq_len, :] = (y * inv * norm[...]).astype(jnp.bfloat16)
 
-    def attend(n):
-        cols = pl.ds(pl.multiple_of(n * tile, tile), tile)
+    def queries(n):
+        cols = pl.ds(n * tile if isinstance(n, int) else pl.multiple_of(n * tile, tile), tile)
         x = xs[...]
-        qt, kt, vt = (jnp.dot(x, w[:, cols], preferred_element_type=jnp.float32).astype(jnp.bfloat16) for w in (wq, wk, wv))
-        for hd in range(tile // HEAD_DIM):
-            hs = slice(hd * HEAD_DIM, (hd + 1) * HEAD_DIM)
-            scores = lax.dot_general(qt[:, hs], kt[:, hs], (((1,), (1,)), ((), ())), preferred_element_type=jnp.float32)
-            scores = jnp.where(causal, scores * (HEAD_DIM ** -0.5), -1e30)
-            raised = jnp.exp(scores - jnp.max(scores, axis=-1, keepdims=True))
-            probs = (raised / jnp.sum(raised, axis=-1, keepdims=True)).astype(jnp.bfloat16)
-            mixed = jnp.dot(probs, vt[:, hs], preferred_element_type=jnp.float32).astype(jnp.bfloat16)
-            mix[:, pl.ds(pl.multiple_of(n * tile + hd * HEAD_DIM, HEAD_DIM), HEAD_DIM)] = mixed
+        return [jnp.dot(x, w[:, cols], preferred_element_type=jnp.float32).astype(jnp.bfloat16) for w in (wq, wk, wv)]
+
+    def attend(n, qkv):
+        cols = pl.ds(n * tile if isinstance(n, int) else pl.multiple_of(n * tile, tile), tile)
+        qt, kt, vt = qkv
+        heads = [slice(hd * HEAD_DIM, (hd + 1) * HEAD_DIM) for hd in range(tile // HEAD_DIM)]
+        scores = jnp.concatenate([lax.dot_general(qt[:, hs], kt[:, hs], (((1,), (1,)), ((), ())),
+                                                  preferred_element_type=jnp.float32) for hs in heads], axis=0)
+        scores = jnp.where(causal, scores * (HEAD_DIM ** -0.5), -1e30)
+        raised = jnp.exp(scores - jnp.max(scores, axis=-1, keepdims=True))
+        probs = (raised / jnp.sum(raised, axis=-1, keepdims=True)).astype(jnp.bfloat16)
+        mixed = [jnp.dot(probs[i * n_tok:(i + 1) * n_tok], vt[:, hs], preferred_element_type=jnp.float32)
+                 for i, hs in enumerate(heads)]
+        mix[:, cols] = jnp.concatenate(mixed, axis=1).astype(jnp.bfloat16)
+
+    def store(c):
+        return pltpu.make_async_copy(hbuf.at[c], z_ref.at[:, pl.ds(pl.multiple_of(c * half, 128), half)], zs.at[c])
 
     def project(q):
         @pl.loop(0, CORES)
@@ -293,8 +302,9 @@
                     rs = pl.ds(b * seq_len, seq_len)
                     hbuf[c, rs, cols] = jnp.where(home == q, z[0], jnp.where(home == q + n_half, z[1], hbuf[c, rs, cols]))
 
-    def store(c):
-        return pltpu.make_async_copy(hbuf.at[c], z_ref.at[:, pl.ds(c * half, half)], zs.at[c])
+            @pl.when(q == n_half - 1)
+            def _():
+                store(c).start()
 
     def last(q):
         for d in range(2):
@@ -333,6 +343,12 @@
         def _():
             first(2)
 
+        for i in range(2, 4):
+            @pl.when(it == i - 1)
+            def _():
+                for part in range(n_half):
+                    weight(i, part).start()
+
         @pl.when(it == 3)
         def _():
             norm_copy.wait()
@@ -345,11 +361,18 @@
         def _():
             normalise(it - 3)
 
+        @pl.when(it == n_half + 2)
+        def _():
+            ahead = queries(0)
+            for n in range(n_sub):
+                now, ahead = ahead, queries(n + 1) if n + 1 < n_sub else None
+                attend(n, now)
+
         @pl.loop(0, n_sub)
         def _(n):
-            @pl.when(it >= 3)
+            @pl.when(jnp.logical_and(it >= 3, it < n_half + 2))
             def _():
-                attend(n)
+                attend(n, queries(n))
 
             @pl.when(jnp.logical_and(it >= 2, it < n_half + 2))
             def _():
@@ -380,9 +403,6 @@
         @pl.when(it == 4)
         def _():
             last(3)
-
-    for c in range(CORES):
-        store(c).start()
 
     @pl.loop(0, n_half)
     def _(q):

time: 109 us -> 103 us (0.945)
  Pallas kernels: 107 us -> 101 us
    pallas_call x1, Pallas kernels: 107 us -> 101 us  [device_step(): pl.pallas_call(functools.partial(stage_kernel, dims), out_shape=jax.Shape...]
where the time goes in v8:
time: 103 us
  Pallas kernels  101 us (98%)
  local copies, waits for them, and re-layouts  2.3 us (2%)
    pallas_call x1, Pallas kernels, device_step(): pl.pallas_call(functools.partial(stage_kernel, dims), out_shape=jax.Shape...  101 us
    unnamed x1, local copies, waits for them, and re-layouts  2.3 us

profile of v8, /device:TPU:97, one launch (start us, length us, event | category | flops | bytes accessed | tf_op | source)
XLA Modules:
  0.0 102.9 jit_solution(14045937813784669570)
XLA Ops:
  0.0 100.5 %stage.1 = bf16[256,2048]{1,0:T(8,128)(2,1)} custom-call(s32[1,64]{1,0:T(1,128)} %owner_ref.1, s32[8,256]{1,0:T(8,128)} %bitcast.23, s32[8,256]{1,0:T(8,128)} %bitcast.24, f32[8,256]{1,0:T(8,128)} %bitcast.25, bf16[8,320,2048]{2,1,0:T(8,128)(2,1)} %bitcast.16, bf16[256,2048]{1,0:T(8,128)(2,1)} %bitcast.22, f32[1,2048]{1,0:T(1,128)} %norm_ref.1, ...), custom_call_target="tpu_custom_call" | custom-call | tf_op jit(solution)/shard_map/stage/pallas_call | solution.py:448
  100.5 2.3 %copy.13 = bf16[1,1,256,2048]{3,2,1,0:T(8,128)(2,1)} copy(bf16[1,1,256,2048]{3,2,1,0:T(8,128)(2,1)} %bitcast.21) | data formatting | bytes 2097152

commit v9 on v8

--- a/solution.py
+++ b/solution.py
@@ -63,11 +63,11 @@
     norm_copy.start()
     comes_copy = pltpu.make_async_copy(owner_ref, comes, c_loc)
     comes_copy.start()
-    for h in order[2:]:
-        o_in(h).start()
-    for i in range(2):
-        for part in range(n_half):
-            weight(i, part).start()
+    def fill(first, stop):
+        for i in range(first, stop):
+            weight(i // n_half, i % n_half).start()
+
+    fill(0, 3)
     if slot_pad > cap:
         for h in range(n_ep):
             obuf[h, :, cap:, :] = jnp.zeros((CORES * n_loc, slot_pad - cap, half), jnp.bfloat16)
@@ -97,9 +97,13 @@
         o_out(n_half * ab).start()
     h_out.start()
 
+    fill(3, 7)
     w_out.wait_recv()
     goes_copy = pltpu.make_async_copy(owners, goes, w_loc)
     goes_copy.start()
+    for h in order[2:4]:
+        o_in(h).start()
+    fill(7, 9)
     goes_copy.wait()
 
     def o_wait(h):
@@ -285,26 +289,34 @@
     def store(c):
         return pltpu.make_async_copy(hbuf.at[c], z_ref.at[:, pl.ds(pl.multiple_of(c * half, 128), half)], zs.at[c])
 
+    def project_tile(q, c, n):
+        def at(start):
+            return pl.ds(start if isinstance(start, int) else pl.multiple_of(start, tile), tile)
+
+        cols = at(c * half + n * tile)
+        out = jnp.dot(mix[...], wo[:, cols], preferred_element_type=jnp.float32).astype(jnp.bfloat16).astype(jnp.float32)
+        z = []
+        for ab in range(2):
+            y = yland[2 * q + ab, :, cols].astype(jnp.float32)
+            z.append((y + out[ab * seq_len:(ab + 1) * seq_len]).astype(jnp.bfloat16))
+        cols = at(n * tile)
+        for b in range(n_ep):
+            home = comes[0, me * n_ep + b] // n_ep
+            rs = pl.ds(b * seq_len, seq_len)
+            hbuf[c, rs, cols] = jnp.where(home == q, z[0], jnp.where(home == q + n_half, z[1], hbuf[c, rs, cols]))
+
     def project(q):
         @pl.loop(0, CORES)
         def _(c):
             @pl.loop(0, half // tile)
             def _(n):
-                cols = pl.ds(pl.multiple_of(c * half + n * tile, tile), tile)
-                out = jnp.dot(mix[...], wo[:, cols], preferred_element_type=jnp.float32).astype(jnp.bfloat16).astype(jnp.float32)
-                z = []
-                for ab in range(2):
-                    y = yland[2 * q + ab, :, cols].astype(jnp.float32)
-                    z.append((y + out[ab * seq_len:(ab + 1) * seq_len]).astype(jnp.bfloat16))
-                cols = pl.ds(pl.multiple_of(n * tile, tile), tile)
-                for b in range(n_ep):
-                    home = comes[0, me * n_ep + b] // n_ep
-                    rs = pl.ds(b * seq_len, seq_len)
-                    hbuf[c, rs, cols] = jnp.where(home == q, z[0], jnp.where(home == q + n_half, z[1], hbuf[c, rs, cols]))
-
-            @pl.when(q == n_half - 1)
-            def _():
-                store(c).start()
+                project_tile(q, c, n)
+
+    def project_last():
+        for c in range(CORES):
+            for n in range(half // tile):
+                project_tile(n_half - 1, c, n)
+            store(c).start()
 
     def last(q):
         for d in range(2):
@@ -343,11 +355,18 @@
         def _():
             first(2)
 
-        for i in range(2, 4):
-            @pl.when(it == i - 1)
-            def _():
-                for part in range(n_half):
-                    weight(i, part).start()
+        @pl.when(it == 0)
+        def _():
+            for h in order[4:]:
+                o_in(h).start()
+
+        @pl.when(it == 1)
+        def _():
+            fill(9, 12)
+
+        @pl.when(it == 2)
+        def _():
+            fill(12, 16)
 
         @pl.when(it == 3)
         def _():
@@ -396,9 +415,13 @@
             def _(h):
                 o_out_wait(h)
 
-        @pl.when(it >= 3)
+        @pl.when(jnp.logical_and(it >= 3, it < n_half + 2))
         def _():
             project(it - 3)
+
+        @pl.when(it == n_half + 2)
+        def _():
+            project_last()
 
         @pl.when(it == 4)
         def _():

time: 103 us -> 103 us (level)
  no operation moved by 1% of the time
where the time goes in v9:
time: 103 us
  Pallas kernels  100 us (97%)
  local copies, waits for them, and re-layouts  2.3 us (2%)
    pallas_call x1, Pallas kernels, device_step(): pl.pallas_call(functools.partial(stage_kernel, dims), out_shape=jax.Shape...  100 us
    unnamed x1, local copies, waits for them, and re-layouts  2.3 us

profile of v9, /device:TPU:97, one launch (start us, length us, event | category | flops | bytes accessed | tf_op | source)
XLA Modules:
  0.0 102.5 jit_solution(17121404921731192181)
XLA Ops:
  0.0 100.2 %stage.1 = bf16[256,2048]{1,0:T(8,128)(2,1)} custom-call(s32[1,64]{1,0:T(1,128)} %owner_ref.1, s32[8,256]{1,0:T(8,128)} %bitcast.23, s32[8,256]{1,0:T(8,128)} %bitcast.24, f32[8,256]{1,0:T(8,128)} %bitcast.25, bf16[8,320,2048]{2,1,0:T(8,128)(2,1)} %bitcast.16, bf16[256,2048]{1,0:T(8,128)(2,1)} %bitcast.22, f32[1,2048]{1,0:T(1,128)} %norm_ref.1, ...), custom_call_target="tpu_custom_call" | custom-call | tf_op jit(solution)/shard_map/stage/pallas_call | solution.py:471
  100.2 2.3 %copy.13 = bf16[1,1,256,2048]{3,2,1,0:T(8,128)(2,1)} copy(bf16[1,1,256,2048]{3,2,1,0:T(8,128)(2,1)} %bitcast.21) | data formatting | bytes 2097152

commit v10 on v9

--- a/solution.py
+++ b/solution.py
@@ -122,7 +122,8 @@
     width = min(256, half)
     tile = min(512, half)
     n_sub = model // tile
-    leg = half // n_sub
+    per_seq = n_sub // CORES
+    leg = seq_len // per_seq
     lane = lax.broadcasted_iota(jnp.int32, (seq_len, depth), 1).astype(jnp.float32)
     block = CORES * seq_len
     per = n_chip * CORES // 2
@@ -228,13 +229,13 @@
         return pl.ds(pl.multiple_of(n * leg, leg), leg)
 
     def last_leg(d, q, n):
-        return pltpu.make_async_remote_copy(r1.at[d, q, :, sub(n)], r3.at[d, q, :, sub(n)], s3.at[d, q, n], q3.at[d, q, n],
+        return pltpu.make_async_remote_copy(r1.at[d, q, sub(n)], r3.at[d, q, sub(n)], s3.at[d, q, n], q3.at[d, q, n],
                                             device_id={'ep': side[d]}, device_id_type=MESH)
 
-    def hop(q, jc, n, c, to):
-        cols = pl.ds(pl.multiple_of(c * half + n * leg, leg), leg)
-        return pltpu.make_async_remote_copy(ysend.at[q, jc, :, :, sub(n)], yland.at[pl.ds(2 * q, 2), :, cols],
-                                            ys.at[q, jc, n], yr.at[c, q, n],
+    def hop(q, jc, m, c, to):
+        return pltpu.make_async_remote_copy(ysend.at[q, jc, :, sub(m)],
+                                            yland.at[pl.ds(2 * q, 2), sub(m), pl.ds(pl.multiple_of(c * half, 128), half)],
+                                            ys.at[q, jc, m], yr.at[c, q, m],
                                             device_id={'pp': nxt, 'ep': to}, device_id_type=MESH)
 
     def finish(q, n):
@@ -242,16 +243,14 @@
         def _():
             for d in range(2):
                 ring(p2, r2, s2, q2, d, q).wait_recv()
-        cols = sub(n)
+        rows = sub(n)
+        jc, m = lax.div(n, per_seq), lax.rem(n, per_seq)
         for d in range(2):
             last_leg(d, q, n).wait_recv()
         for ab in range(2):
-            total = own[ab, lax.rem(q, 3), :, cols] + (r3[ab, q, :, cols] + r2[1 - ab, q, :, cols])
-            rounded = total.astype(jnp.bfloat16)
-            for jc in range(CORES):
-                ysend[q, jc, ab, :, cols] = rounded[jc * seq_len:(jc + 1) * seq_len]
-        for jc in range(CORES):
-            hop(q, jc, n, core, chip * CORES + jc).start()
+            total = own[ab, lax.rem(q, 3), rows] + (r3[ab, q, rows] + r2[1 - ab, q, rows])
+            ysend[q, jc, ab, sub(m)] = total.astype(jnp.bfloat16)
+        hop(q, jc, m, core, chip * CORES + jc).start()
 
     n_tok = 2 * seq_len
     n_row = tile // HEAD_DIM * n_tok
@@ -261,8 +260,8 @@
 
     def normalise(q):
         for c in range(CORES):
-            for n in range(n_sub):
-                hop(q, 0, n, c, me).wait_recv()
+            for m in range(per_seq):
+                hop(q, 0, m, c, me).wait_recv()
         for ab in range(2):
             y = yland[2 * q + ab].astype(jnp.float32)
             inv = lax.rsqrt(jnp.mean(y * y, axis=-1, keepdims=True) + NORM_EPS)
@@ -435,8 +434,8 @@
             for n in range(n_sub):
                 last_leg(d, q, n).wait_send()
         for jc in range(CORES):
-            for n in range(n_sub):
-                hop(q, jc, n, core, chip * CORES + jc).wait_send()
+            for m in range(per_seq):
+                hop(q, jc, m, core, chip * CORES + jc).wait_send()
     for c in range(CORES):
         store(c).wait()
 
@@ -497,7 +496,7 @@
                 dma, dma, dma,
                 dma((2, n_half)), dma((2, n_half)), dma((2, n_half, n_sub)),
                 dma((2, n_half)), dma((2, n_half)), dma((2, n_half, n_sub)),
-                dma((n_half, CORES, n_sub)), dma((CORES, n_half, n_sub)), dma((4, n_half)), dma((CORES,)), dma, dma,
+                dma((n_half, CORES, n_sub // CORES)), dma((CORES, n_half, n_sub // CORES)), dma((4, n_half)), dma((CORES,)), dma, dma,
             ],
             compiler_params=pltpu.CompilerParams(collective_id=0, has_side_effects=True, vmem_limit_bytes=67043328),
             name='stage',

time: 103 us -> 102 us (level)
  no operation moved by 1% of the time
where the time goes in v10:
time: 102 us
  Pallas kernels  99.8 us (98%)
  local copies, waits for them, and re-layouts  2.3 us (2%)
    pallas_call x1, Pallas kernels, device_step(): pl.pallas_call(functools.partial(stage_kernel, dims), out_shape=jax.Shape...  99.8 us
    unnamed x1, local copies, waits for them, and re-layouts  2.3 us

profile of v10, /device:TPU:97, one launch (start us, length us, event | category | flops | bytes accessed | tf_op | source)
XLA Modules:
  0.0 102.1 jit_solution(11812411320316255401)
XLA Ops:
  0.0 99.8 %stage.1 = bf16[256,2048]{1,0:T(8,128)(2,1)} custom-call(s32[1,64]{1,0:T(1,128)} %owner_ref.1, s32[8,256]{1,0:T(8,128)} %bitcast.23, s32[8,256]{1,0:T(8,128)} %bitcast.24, f32[8,256]{1,0:T(8,128)} %bitcast.25, bf16[8,320,2048]{2,1,0:T(8,128)(2,1)} %bitcast.16, bf16[256,2048]{1,0:T(8,128)(2,1)} %bitcast.22, f32[1,2048]{1,0:T(1,128)} %norm_ref.1, ...), custom_call_target="tpu_custom_call" | custom-call | tf_op jit(solution)/shard_map/stage/pallas_call | solution.py:470
  99.8 2.3 %copy.13 = bf16[1,1,256,2048]{3,2,1,0:T(8,128)(2,1)} copy(bf16[1,1,256,2048]{3,2,1,0:T(8,128)(2,1)} %bitcast.21) | data formatting | bytes 2097152
